TPU v7x, 256 devices: a whole 4x4x8 slice. The times are simulated.
256 devices in a mesh: rows: 128 (over z_hi, x, y, core), spec: 2 (over z_lo).
Axes of the slice: x: 4, y: 4, z: 8 (z_hi: 4, z_lo: 2; z = z_hi * 2 + z_lo), core: 2. Of those that a mesh axis runs over, the one named last changes fastest.
Arguments:
- field: float32 [36, 30, 65536], P('spec', None, 'rows'), may hold values from 0.1 to 4
- group_speed: float32 [30], replicated, may hold values from 0.3 to 1
- face_angle: float32 [131072], P('rows'), may hold values from -3.140625 to 3.140625
- face_speed: float32 [131072], P('rows'), may hold values from 0.04 to 0.2
- face_cells: int32 [2, 131072], P(None, 'rows'), may hold values from 0 to 1023, as said below
- face_live: int32 [128], P('rows'), may hold values from 1 to 8, as said below
- halo_blocks: int32 [128, 2, 2], P('rows'), may hold values from 0 to 3
- cell_level: int32 [65536], P('rows'), may hold values from 0 to 2
- polar_mask: int32 [65536], P('rows'), may hold values 0 or 1
- turn_rate: float32 [65536], P('rows'), may hold values from -0.45 to 0.45
Outputs:
- advanced: float32 [36, 30, 65536], P('spec', None, 'rows')
Inputs may be any that keep to these rules, and one draw needn't show every extreme that they name: `face_cells`: row 0 is a face's lower cell, a position among its row block's own 512 cells; row 1 its upper cell, a position among the own cells followed by 2 halo blocks from the block before and 2 from the block after (128 cells each). Only the first face_live[r] of row block r's 8 face blocks carry faces; some row block has all 8 live.
All inputs are finite; a program needn't handle non-finite values. No bound on the sum of `polar_mask` on one device may be relied on, other than what follows from the above.
Results may differ from a plain program's by a relative error of at most 0.0003.
Values sent between devices are 32-bit elements; how exact they have to be, the bound alone decides.
A program may use at most 64 MiB of HBM per device.

v0:
```python
import math

import jax
import jax.numpy as jnp
from jax import lax
from jax.sharding import PartitionSpec as P

NDIR = 36
ITERS = 3


def with_halo(x, sides, width, wrap):
    for axis, dim in sides:
        size, length = (lax.axis_size(axis), x.shape[dim])
        up = [(i, (i + 1) % size) for i in range(size if wrap else size - 1)]
        down = [(j, i) for i, j in up]
        last = lax.slice_in_dim(x, length - width, length, axis=dim)
        first = lax.slice_in_dim(x, 0, width, axis=dim)
        before = lax.ppermute(last, axis, up)
        after = lax.ppermute(first, axis, down)
        x = jnp.concatenate([before, x, after], axis=dim)
    return x


def from_behind(value, axis, steps):
    count = lax.axis_size(axis)
    first, last = (max(0, -steps), min(count, count - steps))
    return lax.ppermute(value, axis, [(source, source + steps) for source in range(first, last)])


def pick_blocks(neighbour, table):
    ndir, nfreq, cdev = neighbour.shape
    view = neighbour.reshape(ndir, nfreq, cdev // 128, 128)
    return jnp.take(view, table, axis=2).reshape(ndir, nfreq, -1)


def block_flux(spectra, own_cells, own_hot, up_hot, signed_hot, forward, backward):
    low_vals = jnp.dot(
        spectra[:, :own_cells],
        own_hot,
        precision=lax.Precision.HIGHEST,
        preferred_element_type=jnp.float32,
    )
    up_vals = jnp.dot(
        spectra, up_hot, precision=lax.Precision.HIGHEST, preferred_element_type=jnp.float32
    )
    flux = forward * low_vals + backward * up_vals
    return lax.dot_general(
        flux,
        signed_hot,
        (((1,), (1,)), ((), ())),
        precision=lax.Precision.HIGHEST,
        preferred_element_type=jnp.float32,
    )


def on_device(
    field,
    group_speed,
    face_angle,
    face_speed,
    face_cells,
    face_live,
    halo_blocks,
    cell_level,
    polar_mask,
    turn_rate,
):
    dloc, nfreq, cdev = field.shape
    fdev = face_angle.shape[0]
    first_dir = lax.axis_index("spec") * dloc
    theta = ((first_dir + jnp.arange(dloc, dtype=jnp.int32)).astype(jnp.float32) + 0.5) * (
        2.0 * math.pi / NDIR
    )
    weight_turn = (polar_mask.astype(jnp.float32) * turn_rate)[None, None, :]
    area_scale = jnp.exp2(-cell_level.astype(jnp.float32))[None, None, :]
    live_count = face_live[0]
    slot_live = (jnp.arange(fdev, dtype=jnp.int32) < live_count * 128).astype(jnp.float32)
    slot_weight = face_speed * slot_live
    lower_all = face_cells[0]
    upper_all = face_cells[1]
    table = halo_blocks[0]
    ext_cells = cdev + 256 * table.shape[1]
    own_hot = (jnp.arange(cdev, dtype=jnp.int32)[:, None] == lower_all[None, :]).astype(jnp.float32)
    up_hot = (jnp.arange(ext_cells, dtype=jnp.int32)[:, None] == upper_all[None, :]).astype(
        jnp.float32
    )
    signed_hot = own_hot - up_hot[:cdev]
    cosine = jnp.cos(theta[:, None] - face_angle[None, :]) * slot_weight[None, :]
    velocity = (group_speed[None, :, None] * cosine[:, None, :]).reshape(dloc * nfreq, fdev)
    forward = jnp.maximum(velocity, 0.0)
    backward = jnp.minimum(velocity, 0.0)
    requests = with_halo(halo_blocks, (("rows", 0),), 1, False)
    wanted_above = requests[2, 0]
    wanted_below = requests[0, 1]
    current = field
    for step in range(ITERS):
        send_up = pick_blocks(current, wanted_above)
        send_down = pick_blocks(current, wanted_below)
        from_below = from_behind(send_up, "rows", 1)
        from_above = from_behind(send_down, "rows", -1)
        extended = jnp.concatenate([current, from_below, from_above], axis=2)
        spectra = extended.reshape(dloc * nfreq, extended.shape[2])
        total = block_flux(spectra, cdev, own_hot, up_hot, signed_hot, forward, backward)
        moved = current - total.reshape(dloc, nfreq, cdev) * area_scale
        rims = with_halo(moved, (("spec", 0),), 1, True)
        before = rims[:-2]
        after = rims[2:]
        current = (
            moved
            - jnp.maximum(weight_turn, 0.0) * (moved - before)
            - jnp.minimum(weight_turn, 0.0) * (after - moved)
        )
    return current


def solution(mesh):
    return jax.shard_map(
        on_device,
        mesh=mesh,
        in_specs=(
            P("spec", None, "rows"),
            P(),
            P("rows"),
            P("rows"),
            P(None, "rows"),
            P("rows"),
            P("rows", None, None),
            P("rows"),
            P("rows"),
            P("rows"),
        ),
        out_specs=P("spec", None, "rows"),
        check_vma=False,
    )
```

profile of v0, /device:TPU:95, one launch (start us, length us, event | category | flops | bytes accessed | tf_op | source)
XLA Modules:
  0.0 221.4 jit_solution(7232645918933782738)
XLA Ops:
  0.0 6.2 %collective-permute-start.2 = (s32[1,2,2]{2,1,0:T(2,128)}, s32[1,2,2]{2,1,0:T(2,128)S(1)}, u32[]{:S(2)}, u32[]{:S(2)}) collective-permute-start(s32[1,2,2]{2,1,0:T(2,128)} %param.18), channel_id=1, source_target_pairs={{0,2},{2,4},{4,6},{6,8},{8,10},{10,12},{12,14},{14,16},{16,18},{18... | collective-permute-start | bytes 56 | tf_op jit(solution)/shard_map/ppermute | solution.py:19
  11.7 6.0 %collective-permute-done = s32[1,2,2]{2,1,0:T(2,128)S(1)} collective-permute-done((s32[1,2,2]{2,1,0:T(2,128)}, s32[1,2,2]{2,1,0:T(2,128)S(1)}, u32[]{:S(2)}, u32[]{:S(2)}) %collective-permute-start) | collective-permute-done | bytes 48 | tf_op jit(solution)/shard_map/ppermute | solution.py:20
  22.6 4.5 %collective-permute-start.1 = (f32[18,30,256]{2,1,0:T(8,128)}, f32[18,30,256]{2,1,0:T(8,128)}, u32[]{:S(2)}, u32[]{:S(2)}) collective-permute-start(f32[18,30,256]{2,1,0:T(8,128)} %reshape.108), channel_id=1, source_target_pairs={{0,2},{2,4},{4,6},{6,8},{8,10},{10,12},{12,14},{14,16},{16,18},{18... | collective-permute-start | bytes 1658888 | tf_op jit(solution)/shard_map/ppermute | solution.py:28
  34.8 5.8 %collective-permute-done.1 = f32[18,30,256]{2,1,0:T(8,128)} collective-permute-done((f32[18,30,256]{2,1,0:T(8,128)}, f32[18,30,256]{2,1,0:T(8,128)}, u32[]{:S(2)}, u32[]{:S(2)}) %collective-permute-start.1) | collective-permute-done | bytes 552992 | tf_op jit(solution)/shard_map/ppermute | solution.py:28
  40.6 9.4 %collective-permute-done.3 = f32[18,30,256]{2,1,0:T(8,128)} collective-permute-done((f32[18,30,256]{2,1,0:T(8,128)}, f32[18,30,256]{2,1,0:T(8,128)}, u32[]{:S(2)}, u32[]{:S(2)}) %collective-permute-start.3) | collective-permute-done | bytes 552992 | tf_op jit(solution)/shard_map/ppermute | solution.py:28
  50.0 2.9 %pad_maximum_fusion = f32[18,30,1024]{2,1,0:T(8,128)} fusion(f32[18,30,256]{2,1,0:T(8,128)} %collective-permute-done.3, f32[18,30,256]{2,1,0:T(8,128)} %collective-permute-done.1, f32[18,30,512]{2,1,0:T(8,128)S(1)} %copy-done.2), kind=kLoop, calls=%fused_computation.10 | loop fusion | flops 1105920 | bytes 4423680 | tf_op jit(solution)/shard_map/concatenate | solution.py:102
  53.0 3.0 %reshape.110 = f32[540,1024]{1,0:T(8,128)} reshape(f32[18,30,1024]{2,1,0:T(8,128)} %pad_maximum_fusion) | data formatting | bytes 4423680 | tf_op jit(solution)/shard_map/reshape | solution.py:103
  55.9 5.6 %fusion.2 = f32[540,1024]{1,0:T(8,128)S(1)} fusion(f32[540,1024]{1,0:T(8,128)} %reshape.110, s32[1024]{0:T(1024)S(1)} %bitcast.31), kind=kOutput, calls=%fused_computation.9 | convolution fusion | flops 6795821056 | bytes 4427776 | tf_op jit(solution)/shard_map/dot_general | solution.py:44
  63.7 4.6 %fusion.11 = f32[540,512]{1,0:T(8,128)S(1)} fusion(f32[540,1024]{1,0:T(8,128)S(1)} %fusion.2, f32[540,1024]{1,0:T(8,128)S(1)} %fusion.20, f32[540,1024]{1,0:T(8,128)S(1)} %mul.143, f32[540]{0:T(1024)S(1)} %mul.133, pred[1024,1024]{1,0:T(32,128)(4,1)S(1)} %copy-done.3, s32[1024]{0:T(1024)S(1)} %bitcast.25), kind=kOutput, calls=%fused_computation.21 | convolution fusion | flops 3402801152 | bytes 8323072 | tf_op jit(solution)/shard_map/dot_general | solution.py:48
  77.7 2.6 %reshape.112 = f32[18,30,4,128]{3,2,1,0:T(4,128)} reshape(f32[18,30,512]{2,1,0:T(8,128)} %fusion.35) | data formatting | bytes 2211840 | tf_op jit(solution)/shard_map/reshape | solution.py:33
  80.4 2.5 %copy.15 = f32[18,30,4,128]{3,1,2,0:T(8,128)} copy(f32[18,30,4,128]{3,2,1,0:T(4,128)} %reshape.112) | data formatting | bytes 2211840 | tf_op jit(solution)/shard_map/reshape | solution.py:33
  82.8 2.8 %gather_fusion.3 = f32[2,18,30,128]{3,2,1,0:T(8,128)} fusion(f32[18,30,4,128]{3,1,2,0:T(8,128)} %copy.15, s32[1024]{0:T(1024)} %copy-done.17), kind=kCustom, calls=%fused_computation.3.clone | custom fusion | bytes 1105928 | tf_op jit(solution)/shard_map/jit(_take)/gather | solution.py:34
  85.6 2.8 %gather_fusion.2 = f32[2,18,30,128]{3,2,1,0:T(8,128)} fusion(f32[18,30,4,128]{3,1,2,0:T(8,128)} %copy.15, s32[1024]{0:T(1024)} %copy-done.18), kind=kCustom, calls=%fused_computation.2.clone | custom fusion | bytes 1105928 | tf_op jit(solution)/shard_map/jit(_take)/gather | solution.py:34
  94.6 2.3 %reshape.113 = f32[18,30,256]{2,1,0:T(8,128)} reshape(f32[18,30,2,128]{3,2,1,0:T(2,128)} %copy.16) | data formatting | bytes 1105920 | tf_op jit(solution)/shard_map/reshape | solution.py:34
  97.0 3.1 %collective-permute-start.6 = (f32[18,30,256]{2,1,0:T(8,128)}, f32[18,30,256]{2,1,0:T(8,128)S(1)}, u32[]{:S(2)}, u32[]{:S(2)}) collective-permute-start(f32[18,30,256]{2,1,0:T(8,128)} %reshape.113), channel_id=1, source_target_pairs={{0,2},{2,4},{4,6},{6,8},{8,10},{10,12},{12,14},{14,16},{16,18},{18... | collective-permute-start | bytes 1658888 | tf_op jit(solution)/shard_map/ppermute | solution.py:28
  102.4 10.9 %collective-permute-done.6 = f32[18,30,256]{2,1,0:T(8,128)S(1)} collective-permute-done((f32[18,30,256]{2,1,0:T(8,128)}, f32[18,30,256]{2,1,0:T(8,128)S(1)}, u32[]{:S(2)}, u32[]{:S(2)}) %collective-permute-start.6) | collective-permute-done | bytes 552992 | tf_op jit(solution)/shard_map/ppermute | solution.py:28
  113.3 10.9 %collective-permute-done.7 = f32[18,30,256]{2,1,0:T(8,128)S(1)} collective-permute-done((f32[18,30,256]{2,1,0:T(8,128)}, f32[18,30,256]{2,1,0:T(8,128)S(1)}, u32[]{:S(2)}, u32[]{:S(2)}) %collective-permute-start.7) | collective-permute-done | bytes 552992 | tf_op jit(solution)/shard_map/ppermute | solution.py:28
  124.2 2.9 %pad_maximum_fusion.1 = f32[18,30,1024]{2,1,0:T(8,128)} fusion(f32[18,30,256]{2,1,0:T(8,128)S(1)} %collective-permute-done.7, f32[18,30,256]{2,1,0:T(8,128)S(1)} %collective-permute-done.6, f32[18,30,512]{2,1,0:T(8,128)} %fusion.35), kind=kLoop, calls=%fused_computation.11 | loop fusion | flops 1105920 | bytes 4423680 | tf_op jit(solution)/shard_map/concatenate | solution.py:102
  127.2 3.0 %reshape.115 = f32[540,1024]{1,0:T(8,128)} reshape(f32[18,30,1024]{2,1,0:T(8,128)} %pad_maximum_fusion.1) | data formatting | bytes 4423680 | tf_op jit(solution)/shard_map/reshape | solution.py:103
  130.2 5.6 %fusion.1 = f32[540,1024]{1,0:T(8,128)S(1)} fusion(f32[540,1024]{1,0:T(8,128)} %reshape.115, s32[1024]{0:T(1024)} %bitcast.32), kind=kOutput, calls=%fused_computation.8 | convolution fusion | flops 6795821056 | bytes 4427776 | tf_op jit(solution)/shard_map/dot_general | solution.py:44
  137.9 5.6 %fusion.7 = f32[540,512]{1,0:T(8,128)} fusion(f32[540,1024]{1,0:T(8,128)S(1)} %fusion.1, f32[540,1024]{1,0:T(8,128)S(1)} %fusion.19, f32[540,1024]{1,0:T(8,128)S(1)} %mul.143, f32[540]{0:T(1024)S(1)} %mul.133, pred[1024,1024]{1,0:T(32,128)(4,1)S(1)} %copy-done.4, s32[1024]{0:T(1024)S(1)} %bitcast.27), kind=kOutput, calls=%fused_computation.17 | convolution fusion | flops 3402801152 | bytes 8323072 | tf_op jit(solution)/shard_map/dot_general | solution.py:48
  143.5 2.4 %reshape.116 = f32[18,30,512]{2,1,0:T(8,128)} reshape(f32[540,512]{1,0:T(8,128)} %fusion.7) | data formatting | bytes 2211840 | tf_op jit(solution)/shard_map/reshape | solution.py:105
  153.5 2.4 %copy.19 = f32[18,30,4,128]{3,1,2,0:T(8,128)} copy(f32[18,30,4,128]{3,2,1,0:T(4,128)} %reshape.117) | data formatting | bytes 2211840 | tf_op jit(solution)/shard_map/reshape | solution.py:33
  155.9 2.8 %gather_fusion.5 = f32[2,18,30,128]{3,2,1,0:T(8,128)} fusion(f32[18,30,4,128]{3,1,2,0:T(8,128)} %copy.19, s32[1024]{0:T(1024)} %copy-done.17), kind=kCustom, calls=%fused_computation.5.clone | custom fusion | bytes 1105928 | tf_op jit(solution)/shard_map/jit(_take)/gather | solution.py:34
  158.7 2.8 %gather_fusion.4 = f32[2,18,30,128]{3,2,1,0:T(8,128)} fusion(f32[18,30,4,128]{3,1,2,0:T(8,128)} %copy.19, s32[1024]{0:T(1024)} %copy-done.18), kind=kCustom, calls=%fused_computation.4.clone | custom fusion | bytes 1105928 | tf_op jit(solution)/shard_map/jit(_take)/gather | solution.py:34
  170.0 2.9 %collective-permute-start.10 = (f32[18,30,256]{2,1,0:T(8,128)}, f32[18,30,256]{2,1,0:T(8,128)S(1)}, u32[]{:S(2)}, u32[]{:S(2)}) collective-permute-start(f32[18,30,256]{2,1,0:T(8,128)} %reshape.118), channel_id=1, source_target_pairs={{0,2},{2,4},{4,6},{6,8},{8,10},{10,12},{12,14},{14,16},{16,18},{18... | collective-permute-start | bytes 1658888 | tf_op jit(solution)/shard_map/ppermute | solution.py:28
  174.9 11.5 %collective-permute-done.10 = f32[18,30,256]{2,1,0:T(8,128)S(1)} collective-permute-done((f32[18,30,256]{2,1,0:T(8,128)}, f32[18,30,256]{2,1,0:T(8,128)S(1)}, u32[]{:S(2)}, u32[]{:S(2)}) %collective-permute-start.10) | collective-permute-done | bytes 552992 | tf_op jit(solution)/shard_map/ppermute | solution.py:28
  186.3 7.3 %collective-permute-done.11 = f32[18,30,256]{2,1,0:T(8,128)S(1)} collective-permute-done((f32[18,30,256]{2,1,0:T(8,128)}, f32[18,30,256]{2,1,0:T(8,128)S(1)}, u32[]{:S(2)}, u32[]{:S(2)}) %collective-permute-start.11) | collective-permute-done | bytes 552992 | tf_op jit(solution)/shard_map/ppermute | solution.py:28
  195.3 3.0 %reshape.120 = f32[540,1024]{1,0:T(8,128)} reshape(f32[18,30,1024]{2,1,0:T(8,128)} %pad_maximum_fusion.2) | data formatting | bytes 4423680 | tf_op jit(solution)/shard_map/reshape | solution.py:103
  198.3 5.6 %fusion = f32[540,1024]{1,0:T(8,128)S(1)} fusion(f32[540,1024]{1,0:T(8,128)} %reshape.120, s32[1024]{0:T(1024)S(1)} %bitcast.33), kind=kOutput, calls=%fused_computation.7 | convolution fusion | flops 6795821056 | bytes 4427776 | tf_op jit(solution)/shard_map/dot_general | solution.py:44
  206.0 4.6 %fusion.3 = f32[540,512]{1,0:T(8,128)S(1)} fusion(f32[540,1024]{1,0:T(8,128)S(1)} %fusion, f32[540,1024]{1,0:T(8,128)S(1)} %fusion.18, f32[540,1024]{1,0:T(8,128)S(1)} %mul.143, f32[540]{0:T(1024)S(1)} %mul.133, pred[1024,1024]{1,0:T(32,128)(4,1)S(1)} %copy-done.5, s32[1024]{0:T(1024)S(1)} %bitcast.29), kind=kOutput, calls=%fused_computation.13 | convolution fusion | flops 3402801152 | bytes 8323072 | tf_op jit(solution)/shard_map/dot_general | solution.py:48
  213.1 3.8 %collective-permute-start.12 = (f32[1,30,512]{2,1,0:T(8,128)S(1)}, f32[1,30,512]{2,1,0:T(8,128)S(1)}, u32[]{:S(2)}, u32[]{:S(2)}) collective-permute-start(f32[1,30,512]{2,1,0:T(8,128)S(1)} %get-tuple-element.10), channel_id=1, source_target_pairs={{0,1},{1,0},{2,3},{3,2},{4,5},{5,4},{6,7},{7,6},{8,9},{9,8},{10,11... | collective-permute-start | bytes 184328 | tf_op jit(solution)/shard_map/ppermute | solution.py:19
  (128 shorter events, 67.7 us)
Async XLA Ops:
  0.0 11.6 %collective-permute-start.2 = (s32[1,2,2]{2,1,0:T(2,128)}, s32[1,2,2]{2,1,0:T(2,128)S(1)}, u32[]{:S(2)}, u32[]{:S(2)}) collective-permute-start(s32[1,2,2]{2,1,0:T(2,128)} %param.18), channel_id=1, source_target_pairs={{0,2},{2,4},{4,6},{6,8},{8,10},{10,12},{12,14},{14,16},{16,18},{18... | collective-permute-start | bytes 56 | tf_op jit(solution)/shard_map/ppermute | solution.py:19
  6.2 11.4 %collective-permute-start = (s32[1,2,2]{2,1,0:T(2,128)}, s32[1,2,2]{2,1,0:T(2,128)S(1)}, u32[]{:S(2)}, u32[]{:S(2)}) collective-permute-start(s32[1,2,2]{2,1,0:T(2,128)} %param.18), channel_id=1, source_target_pairs={{2,0},{4,2},{6,4},{8,6},{10,8},{12,10},{14,12},{16,14},{18,16},{20... | collective-permute-start | bytes 56 | tf_op jit(solution)/shard_map/ppermute | solution.py:20
  11.7 7.8 %copy-start.19 = (pred[2]{0:T(512)(128)(4,1)}, pred[2]{0:T(512)(128)(4,1)S(1)}, u32[]{:S(2)}) copy-start(pred[2]{0:T(512)(128)(4,1)S(1)} %get-tuple-element.8) | copy-start | bytes 10
  11.7 6.0 %copy-start.17 = (s32[1024]{0:T(1024)}, s32[1024]{0:T(1024)S(1)}, u32[]{:S(2)}) copy-start(s32[1024]{0:T(1024)S(1)} %pad_clamp_fusion) | copy-start | bytes 12292
  20.1 9.2 %copy-start.26 = (s32[512]{0:T(512)S(1)}, s32[512]{0:T(512)}, u32[]{:S(2)}) copy-start(s32[512]{0:T(512)} %param.19) | copy-start | bytes 6148
  20.1 9.2 %copy-start.29 = (f32[30]{0:T(128)S(1)}, f32[30]{0:T(128)}, u32[]{:S(2)}) copy-start(f32[30]{0:T(128)} %param.13) | copy-start | bytes 364
  22.6 17.9 %collective-permute-start.1 = (f32[18,30,256]{2,1,0:T(8,128)}, f32[18,30,256]{2,1,0:T(8,128)}, u32[]{:S(2)}, u32[]{:S(2)}) collective-permute-start(f32[18,30,256]{2,1,0:T(8,128)} %reshape.108), channel_id=1, source_target_pairs={{0,2},{2,4},{4,6},{6,8},{8,10},{10,12},{12,14},{14,16},{16,18},{18... | collective-permute-start | bytes 1658888 | tf_op jit(solution)/shard_map/ppermute | solution.py:28
  27.2 22.8 %collective-permute-start.3 = (f32[18,30,256]{2,1,0:T(8,128)}, f32[18,30,256]{2,1,0:T(8,128)}, u32[]{:S(2)}, u32[]{:S(2)}) collective-permute-start(f32[18,30,256]{2,1,0:T(8,128)} %reshape.109), channel_id=1, source_target_pairs={{2,0},{4,2},{6,4},{8,6},{10,8},{12,10},{14,12},{16,14},{18,16},{20... | collective-permute-start | bytes 1658888 | tf_op jit(solution)/shard_map/ppermute | solution.py:28
  29.3 40.1 %copy-start.12 = (f32[512]{0:T(512)}, f32[512]{0:T(512)S(1)}, u32[]{:S(2)}) copy-start(f32[512]{0:T(512)S(1)} %multiply_exponential_fusion) | copy-start | bytes 6148
  31.1 18.9 %copy-start.2 = (f32[18,30,512]{2,1,0:T(8,128)S(1)}, f32[18,30,512]{2,1,0:T(8,128)}, u32[]{:S(2)}) copy-start(f32[18,30,512]{2,1,0:T(8,128)} %param.12) | copy-start | bytes 3317764
  33.0 22.9 %copy-start.14 = (s32[1,1024]{1,0:T(1,128)}, s32[1,1024]{1,0:T(1,128)S(1)}, u32[]{:S(2)}) copy-start(s32[1,1024]{1,0:T(1,128)S(1)} %get-tuple-element.17) | copy-start | bytes 12292
  55.9 5.6 %copy-start.6 = (f32[540,1024]{1,0:T(8,128)S(1)}, f32[540,1024]{1,0:T(8,128)}, u32[]{:S(2)}) copy-start(f32[540,1024]{1,0:T(8,128)} %reshape.110) | copy-start | bytes 6635524
  69.4 4.0 %copy-start.27 = (f32[512]{0:T(512)S(1)}, f32[512]{0:T(512)}, u32[]{:S(2)}) copy-start(f32[512]{0:T(512)} %param.21) | copy-start | bytes 6148
  69.4 4.0 %copy-start.28 = (s32[512]{0:T(512)S(1)}, s32[512]{0:T(512)}, u32[]{:S(2)}) copy-start(s32[512]{0:T(512)} %param.20) | copy-start | bytes 6148
  71.4 3.6 %collective-permute-start.4 = (f32[1,30,512]{2,1,0:T(8,128)S(1)}, f32[1,30,512]{2,1,0:T(8,128)S(1)}, u32[]{:S(2)}, u32[]{:S(2)}) collective-permute-start(f32[1,30,512]{2,1,0:T(8,128)S(1)} %get-tuple-element.14), channel_id=1, source_target_pairs={{0,1},{1,0},{2,3},{3,2},{4,5},{5,4},{6,7},{7,6},{8,9},{9,8},{10,11... | collective-permute-start | bytes 184328 | tf_op jit(solution)/shard_map/ppermute | solution.py:19
  73.3 3.1 %collective-permute-start.5 = (f32[1,30,512]{2,1,0:T(8,128)S(1)}, f32[1,30,512]{2,1,0:T(8,128)S(1)}, u32[]{:S(2)}, u32[]{:S(2)}) collective-permute-start(f32[1,30,512]{2,1,0:T(8,128)S(1)} %get-tuple-element.15), channel_id=1, source_target_pairs={{1,0},{0,1},{3,2},{2,3},{5,4},{4,5},{7,6},{6,7},{9,8},{8,9},{11,10... | collective-permute-start | bytes 184328 | tf_op jit(solution)/shard_map/ppermute | solution.py:20
  88.4 2.5 %copy-start.10 = (f32[2,18,30,128]{3,2,1,0:T(8,128)S(1)}, f32[2,18,30,128]{3,2,1,0:T(8,128)}, u32[]{:S(2)}) copy-start(f32[2,18,30,128]{3,2,1,0:T(8,128)} %gather_fusion.3) | copy-start | bytes 1658884
  88.4 2.5 %copy-start.20 = (pred[2]{0:T(512)(128)(4,1)S(1)}, pred[2]{0:T(512)(128)(4,1)}, u32[]{:S(2)}) copy-start(pred[2]{0:T(512)(128)(4,1)} %copy-done.19) | copy-start | bytes 10
  97.0 16.4 %collective-permute-start.6 = (f32[18,30,256]{2,1,0:T(8,128)}, f32[18,30,256]{2,1,0:T(8,128)S(1)}, u32[]{:S(2)}, u32[]{:S(2)}) collective-permute-start(f32[18,30,256]{2,1,0:T(8,128)} %reshape.113), channel_id=1, source_target_pairs={{0,2},{2,4},{4,6},{6,8},{8,10},{10,12},{12,14},{14,16},{16,18},{18... | collective-permute-start | bytes 1658888 | tf_op jit(solution)/shard_map/ppermute | solution.py:28
  100.1 24.2 %collective-permute-start.7 = (f32[18,30,256]{2,1,0:T(8,128)}, f32[18,30,256]{2,1,0:T(8,128)S(1)}, u32[]{:S(2)}, u32[]{:S(2)}) collective-permute-start(f32[18,30,256]{2,1,0:T(8,128)} %reshape.114), channel_id=1, source_target_pairs={{2,0},{4,2},{6,4},{8,6},{10,8},{12,10},{14,12},{16,14},{18,16},{20... | collective-permute-start | bytes 1658888 | tf_op jit(solution)/shard_map/ppermute | solution.py:28
  130.2 5.6 %copy-start.8 = (f32[540,1024]{1,0:T(8,128)S(1)}, f32[540,1024]{1,0:T(8,128)}, u32[]{:S(2)}) copy-start(f32[540,1024]{1,0:T(8,128)} %reshape.115) | copy-start | bytes 6635524
  147.5 3.9 %copy-start = (f32[18,30,512]{2,1,0:T(8,128)}, f32[18,30,512]{2,1,0:T(8,128)S(1)}, u32[]{:S(2)}) copy-start(f32[18,30,512]{2,1,0:T(8,128)S(1)} %multiply_subtract_fusion.1) | copy-start | bytes 3317764
  147.5 3.2 %collective-permute-start.8 = (f32[1,30,512]{2,1,0:T(8,128)S(1)}, f32[1,30,512]{2,1,0:T(8,128)S(1)}, u32[]{:S(2)}, u32[]{:S(2)}) collective-permute-start(f32[1,30,512]{2,1,0:T(8,128)S(1)} %get-tuple-element.12), channel_id=1, source_target_pairs={{0,1},{1,0},{2,3},{3,2},{4,5},{5,4},{6,7},{7,6},{8,9},{9,8},{10,11... | collective-permute-start | bytes 184328 | tf_op jit(solution)/shard_map/ppermute | solution.py:19
  147.6 3.8 %collective-permute-start.9 = (f32[1,30,512]{2,1,0:T(8,128)S(1)}, f32[1,30,512]{2,1,0:T(8,128)S(1)}, u32[]{:S(2)}, u32[]{:S(2)}) collective-permute-start(f32[1,30,512]{2,1,0:T(8,128)S(1)} %get-tuple-element.13), channel_id=1, source_target_pairs={{1,0},{0,1},{3,2},{2,3},{5,4},{4,5},{7,6},{6,7},{9,8},{8,9},{11,10... | collective-permute-start | bytes 184328 | tf_op jit(solution)/shard_map/ppermute | solution.py:20
  155.9 5.6 %copy-start.23 = (pred[2]{0:T(512)(128)(4,1)S(1)}, pred[2]{0:T(512)(128)(4,1)}, u32[]{:S(2)}) copy-start(pred[2]{0:T(512)(128)(4,1)} %copy-done.22) | copy-start | bytes 10
  161.5 2.5 %copy-start.21 = (pred[2]{0:T(512)(128)(4,1)S(1)}, pred[2]{0:T(512)(128)(4,1)}, u32[]{:S(2)}) copy-start(pred[2]{0:T(512)(128)(4,1)} %copy-done.19) | copy-start | bytes 10
  170.0 16.3 %collective-permute-start.10 = (f32[18,30,256]{2,1,0:T(8,128)}, f32[18,30,256]{2,1,0:T(8,128)S(1)}, u32[]{:S(2)}, u32[]{:S(2)}) collective-permute-start(f32[18,30,256]{2,1,0:T(8,128)} %reshape.118), channel_id=1, source_target_pairs={{0,2},{2,4},{4,6},{6,8},{8,10},{10,12},{12,14},{14,16},{16,18},{18... | collective-permute-start | bytes 1658888 | tf_op jit(solution)/shard_map/ppermute | solution.py:28
  173.0 20.6 %collective-permute-start.11 = (f32[18,30,256]{2,1,0:T(8,128)}, f32[18,30,256]{2,1,0:T(8,128)S(1)}, u32[]{:S(2)}, u32[]{:S(2)}) collective-permute-start(f32[18,30,256]{2,1,0:T(8,128)} %reshape.119), channel_id=1, source_target_pairs={{2,0},{4,2},{6,4},{8,6},{10,8},{12,10},{14,12},{16,14},{18,16},{20... | collective-permute-start | bytes 1658888 | tf_op jit(solution)/shard_map/ppermute | solution.py:28
  195.3 3.0 %copy-start.15 = (s32[1,1024]{1,0:T(1,128)S(1)}, s32[1,1024]{1,0:T(1,128)}, u32[]{:S(2)}) copy-start(s32[1,1024]{1,0:T(1,128)} %copy-done.14) | copy-start | bytes 12292
  198.3 5.6 %copy-start.7 = (f32[540,1024]{1,0:T(8,128)S(1)}, f32[540,1024]{1,0:T(8,128)}, u32[]{:S(2)}) copy-start(f32[540,1024]{1,0:T(8,128)} %reshape.120) | copy-start | bytes 6635524
  213.1 5.5 %collective-permute-start.12 = (f32[1,30,512]{2,1,0:T(8,128)S(1)}, f32[1,30,512]{2,1,0:T(8,128)S(1)}, u32[]{:S(2)}, u32[]{:S(2)}) collective-permute-start(f32[1,30,512]{2,1,0:T(8,128)S(1)} %get-tuple-element.10), channel_id=1, source_target_pairs={{0,1},{1,0},{2,3},{3,2},{4,5},{5,4},{6,7},{7,6},{8,9},{9,8},{10,11... | collective-permute-start | bytes 184328 | tf_op jit(solution)/shard_map/ppermute | solution.py:19
  216.9 3.1 %collective-permute-start.13 = (f32[1,30,512]{2,1,0:T(8,128)S(1)}, f32[1,30,512]{2,1,0:T(8,128)S(1)}, u32[]{:S(2)}, u32[]{:S(2)}) collective-permute-start(f32[1,30,512]{2,1,0:T(8,128)S(1)} %get-tuple-element.11), channel_id=1, source_target_pairs={{1,0},{0,1},{3,2},{2,3},{5,4},{4,5},{7,6},{6,7},{9,8},{8,9},{11,10... | collective-permute-start | bytes 184328 | tf_op jit(solution)/shard_map/ppermute | solution.py:20
  (12 other events, 17.8 us)
where the time goes:
time: 226 us; the launch traced here: 221 us
  waiting for transfers between devices  70 us (31%)
  local copies, waits for them, and re-layouts  59.1 us (26%)
  matrix products  37.9 us (17%)
  starting transfers between devices  32.7 us (14%)
  other arithmetic  20.3 us (9%)
    ppermute x6, waiting for transfers between devices, from_behind(): lax.ppermute(value, axis, [(source, source + steps) for source in range(f...  55.8 us
    dot_general x3, matrix products, block_flux(): jnp.dot(spectra, up_hot, precision=lax.Precision.HIGHEST, preferred_eleme...  16.9 us
    ppermute x6, starting transfers between devices, from_behind(): lax.ppermute(value, axis, [(source, source + steps) for source in range(f...  16.9 us
    dot_general x3, matrix products, block_flux(): lax.dot_general(flux, signed_hot, (((1,), (1,)), ((), ())), precision=lax...  14.8 us
    gather x6, local copies, waits for them, and re-layouts, pick_blocks(): return jnp.take(view, table, axis=2).reshape(ndir, nfreq, -1)  12.4 us
    ppermute x4, starting transfers between devices, with_halo(): before = lax.ppermute(last, axis, up)  12.1 us
    reshape x6, local copies, waits for them, and re-layouts, pick_blocks(): return jnp.take(view, table, axis=2).reshape(ndir, nfreq, -1)  11.8 us
    reshape x6, local copies, waits for them, and re-layouts, pick_blocks(): view = neighbour.reshape(ndir, nfreq, cdev // 128, 128)  10.8 us
  transfers between devices with their start and end apart: 14, of which 13 were waited for; matrix products, arithmetic and copies ran while one was open for 3% of the time, Pallas kernels for 0%

commit v1 on v0

v1 whole, which is shorter than its diff:
```python
import functools
import math

import jax
import jax.numpy as jnp
from jax import lax
from jax.experimental import pallas as pl
from jax.experimental.pallas import tpu as pltpu
from jax.sharding import PartitionSpec as P

MESH = pl.DeviceIdType.MESH
NDIR = 36
ITERS = 3
LANES = 128
ROWS = 32
CHUNK = 3
BF16 = jnp.bfloat16
F32 = jnp.float32


def split(value):
    high = value.astype(BF16)
    return high, (value - high.astype(F32)).astype(BF16)


def kernel(
    field,
    speed_s,
    angle_h,
    weight_h,
    cells_h,
    live_s,
    table_h,
    level_h,
    mask_h,
    rate_h,
    out,
    cur,
    moved,
    sent,
    got,
    edge_sent,
    edge_got,
    ext_hi,
    ext_lo,
    flux_hi,
    flux_lo,
    own_hot,
    up_hot,
    back_hot,
    vel,
    scale,
    turn,
    angle,
    weight,
    cells,
    level,
    mask,
    rate,
    table_v,
    table_r,
    picks,
    load_sem,
    out_sem,
    small_sem,
    table_send,
    table_recv,
    send_sem,
    recv_sem,
    edge_send,
    edge_recv,
):
    dloc, nfreq, own = field.shape
    pairs = dloc // 2
    chunks = pairs // CHUNK
    hb = table_h.shape[2]
    faces = cells.shape[1]
    fblk = faces // LANES
    size = lax.axis_size("rows")
    row = lax.axis_index("rows")
    spec = lax.axis_index("spec")
    has = (row > 0, row < size - 1)
    peer = ({"rows": jnp.maximum(row - 1, 0)}, {"rows": jnp.minimum(row + 1, size - 1)})
    partner = {"spec": 1 - spec}

    def slot(d):
        return 2 * d if d < pairs else 2 * (dloc - 1 - d) + 1

    def direction(p):
        return p // 2 if p % 2 == 0 else dloc - 1 - p // 2

    small = [
        pltpu.make_async_copy(src, dst, small_sem.at[i])
        for i, (src, dst) in enumerate(
            (
                (table_h, table_v),
                (cells_h, cells),
                (angle_h, angle),
                (weight_h, weight),
                (level_h, level),
                (mask_h, mask),
                (rate_h, rate),
            )
        )
    ]
    for copy in small:
        copy.start()
    loads = [
        pltpu.make_async_copy(
            field.at[direction(p)], cur.at[p], load_sem.at[p]
        )
        for p in range(dloc)
    ]
    for copy in loads:
        copy.start()
    table_r[...] = jnp.zeros_like(table_r)

    barrier = pltpu.get_barrier_semaphore()
    pl.semaphore_signal(barrier, inc=1, device_id=partner, device_id_type=MESH)
    for side in (0, 1):

        @pl.when(has[side])
        def _():
            pl.semaphore_signal(barrier, inc=1, device_id=peer[side], device_id_type=MESH)

    pl.semaphore_wait(barrier, 1 + has[0].astype(jnp.int32) + has[1].astype(jnp.int32))

    small[0].wait()
    tables = [
        pltpu.make_async_remote_copy(
            src_ref=table_v,
            dst_ref=table_r.at[1 - side],
            send_sem=table_send.at[side],
            recv_sem=table_recv.at[1 - side],
            device_id=peer[side],
            device_id_type=MESH,
        )
        for side in (0, 1)
    ]
    for side in (0, 1):

        @pl.when(has[side])
        def _():
            tables[side].start()

    for copy in small[1:]:
        copy.wait()

    sub = lax.broadcasted_iota(jnp.int32, (LANES, LANES), 0)
    lane = lax.broadcasted_iota(jnp.int32, (LANES, LANES), 1)
    one = jnp.float32(1.0)
    zero = jnp.float32(0.0)

    def build(j, carry):
        at = pl.ds(pl.multiple_of(j * LANES, LANES), LANES)
        low = jnp.broadcast_to(cells[0:1, at], (LANES, LANES))
        upp = jnp.broadcast_to(cells[1:2, at], (LANES, LANES))
        for c in range(own // LANES):
            own_hot[c * LANES : (c + 1) * LANES, at] = jnp.where(
                low == sub + c * LANES, one, zero
            ).astype(BF16)
        for c in range(up_hot.shape[0] // LANES):
            up_hot[c * LANES : (c + 1) * LANES, at] = jnp.where(
                upp == sub + c * LANES, one, zero
            ).astype(BF16)
        low_t = low.T
        upp_t = upp.T
        for c in range(own // LANES):
            here = lane + c * LANES
            back_hot[at, c * LANES : (c + 1) * LANES] = (
                jnp.where(low_t == here, one, zero) - jnp.where(upp_t == here, one, zero)
            ).astype(BF16)
        return carry

    lax.fori_loop(0, fblk, build, 0)

    blocks = lax.broadcasted_iota(jnp.int32, (fblk, LANES), 0)
    slot_weight = jnp.where(blocks < live_s[0], weight[...], zero)
    along = jnp.cos(angle[...]) * slot_weight
    across = jnp.sin(angle[...]) * slot_weight
    sign = (1 - 2 * spec).astype(F32)
    along = along * sign
    across = across * sign
    for p in range(dloc):
        theta = (direction(p) + 0.5) * (2.0 * math.pi / NDIR)
        vel[p] = along * math.cos(theta) + across * math.sin(theta)

    freq = lax.broadcasted_iota(jnp.int32, (nfreq, LANES), 0)
    group = jnp.zeros((nfreq, LANES), F32)
    for f in range(nfreq):
        group = jnp.where(freq == f, speed_s[f], group)
    for c in range(own // LANES):
        lev = level[0:1, c * LANES : (c + 1) * LANES]
        area = jnp.exp2(-lev.astype(F32))
        scale[:, c * LANES : (c + 1) * LANES] = group * area
    bend = mask[...].astype(F32) * rate[...]
    turn[0:1, :] = jnp.maximum(bend, 0.0)
    turn[1:2, :] = jnp.minimum(bend, 0.0)

    for side in (0, 1):

        @pl.when(jnp.logical_not(has[side]))
        def _():
            def clear(i, carry):
                def inner(j, c):
                    got[i, side, j] = jnp.zeros(got.shape[3:], F32)
                    return c

                return lax.fori_loop(0, pairs, inner, carry)

            lax.fori_loop(0, ITERS, clear, 0)

    for side in (0, 1):

        @pl.when(has[side])
        def _():
            pltpu.make_async_remote_copy(
                src_ref=table_v,
                dst_ref=table_r.at[side],
                send_sem=table_send.at[side],
                recv_sem=table_recv.at[side],
                device_id=peer[side],
                device_id_type=MESH,
            ).wait_recv()

    for side in (0, 1):
        taken = table_r[side, 0]
        for k in range(hb):
            picks[side * hb + k] = jnp.broadcast_to(
                taken[1 - side : 2 - side, k : k + 1], (8, LANES)
            )

    def pick(value, side, k):
        wanted = jnp.broadcast_to(picks[side * hb + k, 0:1, :], (nfreq, LANES))
        chosen = value[:, 0:LANES]
        for c in range(1, own // LANES):
            chosen = jnp.where(wanted == c, value[:, c * LANES : (c + 1) * LANES], chosen)
        return chosen

    def halo_copy(step, side, pair):
        return pltpu.make_async_remote_copy(
            src_ref=sent.at[step, side, pair],
            dst_ref=got.at[step, 1 - side, pair],
            send_sem=send_sem.at[step, side, pair],
            recv_sem=recv_sem.at[step, 1 - side, pair],
            device_id=peer[side],
            device_id_type=MESH,
        )

    def halo_arrival(step, side, pair):
        return pltpu.make_async_remote_copy(
            src_ref=sent.at[step, side, pair],
            dst_ref=got.at[step, side, pair],
            send_sem=send_sem.at[step, side, pair],
            recv_sem=recv_sem.at[step, side, pair],
            device_id=peer[side],
            device_id_type=MESH,
        )

    def send_pair(step, pair):
        for side in (0, 1):
            for e in (0, 1):
                value = cur[2 * pair + e]
                for k in range(hb):
                    sent[step, side, pair, e, k] = pick(value, side, k)

            @pl.when(has[side])
            def _():
                halo_copy(step, side, pair).start()

    def split_own(p):
        rows = pl.ds(p * ROWS, nfreq)
        high, low = split(cur[p])
        ext_hi[rows, 0:own] = high
        ext_lo[rows, 0:own] = low

    for pair in range(pairs):
        for e in (0, 1):
            loads[2 * pair + e].wait()
        send_pair(0, pair)
    for p in range(dloc):
        split_own(p)

    def turn_slot(step, p):
        d = direction(p)
        here = moved[p]
        before = moved[slot(d - 1)] if d > 0 else edge_got[step, 1]
        after = moved[slot(d + 1)] if d < dloc - 1 else edge_got[step, 0]
        cur[p] = here - turn[0:1, :] * (here - before) - turn[1:2, :] * (after - here)
        split_own(p)

    def edge_copy(step):
        return pltpu.make_async_remote_copy(
            src_ref=edge_sent.at[step],
            dst_ref=edge_got.at[step],
            send_sem=edge_send.at[step],
            recv_sem=edge_recv.at[step],
            device_id=partner,
            device_id_type=MESH,
        )

    def store_pair(pair):
        return [
            pltpu.make_async_copy(
                cur.at[p], out.at[direction(p)], out_sem.at[p]
            )
            for p in (2 * pair, 2 * pair + 1)
        ]

    def finish_pair(step, pair):
        turn_slot(step, 2 * pair)
        turn_slot(step, 2 * pair + 1)

        @pl.when(step < ITERS - 1)
        def _():
            send_pair(step + 1, pair)

        @pl.when(step == ITERS - 1)
        def _():
            for copy in store_pair(pair):
                copy.start()

    def compute(step, chunk):
        span = 2 * CHUNK * ROWS
        rows = pl.ds(chunk * span, span)
        for i in range(CHUNK):
            pair = chunk * CHUNK + i
            for side in (0, 1):

                @pl.when(has[side])
                def _():
                    halo_arrival(step, side, pair).wait_recv()

            for side in (0, 1):
                for e in (0, 1):
                    for k in range(hb):
                        high, low = split(got[step, side, pair, e, k])
                        at = pl.ds(own + (side * hb + k) * LANES, LANES)
                        there = pl.ds((2 * pair + e) * ROWS, nfreq)
                        ext_hi[there, at] = high
                        ext_lo[there, at] = low
        width = 2 * LANES
        for n in range(faces // width):
            at = slice(n * width, (n + 1) * width)
            low = jnp.dot(
                ext_hi[rows, 0:own], own_hot[:, at], preferred_element_type=F32
            ) + jnp.dot(ext_lo[rows, 0:own], own_hot[:, at], preferred_element_type=F32)
            upp = jnp.dot(
                ext_hi[rows, :], up_hot[:, at], preferred_element_type=F32
            ) + jnp.dot(ext_lo[rows, :], up_hot[:, at], preferred_element_type=F32)
            for i in range(2 * CHUNK):
                p = chunk * 2 * CHUNK + i
                there = slice(i * ROWS, (i + 1) * ROWS)
                for h in range(2):
                    inner = slice(h * LANES, (h + 1) * LANES)
                    u = jnp.broadcast_to(
                        vel[p, 2 * n + h : 2 * n + h + 1, :], (ROWS, LANES)
                    )
                    flow = u * jnp.where(u > 0.0, low[there, inner], upp[there, inner])
                    high, rest = split(flow)
                    outer = slice(n * width + h * LANES, n * width + (h + 1) * LANES)
                    flux_hi[there, outer] = high
                    flux_lo[there, outer] = rest
        total = jnp.dot(flux_hi[...], back_hot[...], preferred_element_type=F32) + jnp.dot(
            flux_lo[...], back_hot[...], preferred_element_type=F32
        )
        for i in range(2 * CHUNK):
            p = chunk * 2 * CHUNK + i
            moved[p] = cur[p] - scale[...] * total[i * ROWS : i * ROWS + nfreq]

    def one_step(step, carry):
        compute(step, 0)
        edge_sent[step] = moved[0:2]
        edge_copy(step).start()
        finish_pair(step, 1)
        compute(step, 1)
        edge_copy(step).wait_recv()
        for pair in (0, 2, 3, 4):
            finish_pair(step, pair)
        compute(step, 2)
        for pair in (5, 6, 7, 8):
            finish_pair(step, pair)
        return carry

    lax.fori_loop(0, ITERS, one_step, 0)

    for side in (0, 1):

        @pl.when(has[side])
        def _():
            tables[side].wait_send()

    def drain(step, carry):
        edge_copy(step).wait_send()
        for side in (0, 1):

            @pl.when(has[side])
            def _():
                def inner(pair, c):
                    halo_copy(step, side, pair).wait_send()
                    return c

                lax.fori_loop(0, pairs, inner, 0)

        return carry

    lax.fori_loop(0, ITERS, drain, 0)
    for pair in range(pairs):
        for copy in store_pair(pair):
            copy.wait()


def on_device(
    field,
    group_speed,
    face_angle,
    face_speed,
    face_cells,
    face_live,
    halo_blocks,
    cell_level,
    polar_mask,
    turn_rate,
):
    dloc, nfreq, own = field.shape
    faces = face_angle.shape[0]
    fblk = faces // LANES
    hb = halo_blocks.shape[2]
    ext = own + 2 * hb * LANES
    pairs = dloc // 2
    any_spec = pl.BlockSpec(memory_space=pl.ANY)
    smem_spec = pl.BlockSpec(memory_space=pltpu.SMEM)
    halo = (ITERS, 2, pairs, 2, hb, nfreq, LANES)
    span = 2 * CHUNK * ROWS
    return pl.pallas_call(
        kernel,
        out_shape=jax.ShapeDtypeStruct(field.shape, field.dtype),
        in_specs=[
            any_spec,
            smem_spec,
            any_spec,
            any_spec,
            any_spec,
            smem_spec,
            any_spec,
            any_spec,
            any_spec,
            any_spec,
        ],
        out_specs=any_spec,
        scratch_shapes=[
            pltpu.VMEM((dloc, nfreq, own), F32),
            pltpu.VMEM((dloc, nfreq, own), F32),
            pltpu.VMEM(halo, F32),
            pltpu.VMEM(halo, F32),
            pltpu.VMEM((ITERS, 2, nfreq, own), F32),
            pltpu.VMEM((ITERS, 2, nfreq, own), F32),
            pltpu.VMEM((dloc * ROWS, ext), BF16),
            pltpu.VMEM((dloc * ROWS, ext), BF16),
            pltpu.VMEM((span, faces), BF16),
            pltpu.VMEM((span, faces), BF16),
            pltpu.VMEM((own, faces), BF16),
            pltpu.VMEM((ext, faces), BF16),
            pltpu.VMEM((faces, own), BF16),
            pltpu.VMEM((dloc, fblk, LANES), F32),
            pltpu.VMEM((nfreq, own), F32),
            pltpu.VMEM((2, own), F32),
            pltpu.VMEM((fblk, LANES), F32),
            pltpu.VMEM((fblk, LANES), F32),
            pltpu.VMEM((2, faces), jnp.int32),
            pltpu.VMEM((1, own), jnp.int32),
            pltpu.VMEM((1, own), jnp.int32),
            pltpu.VMEM((1, own), F32),
            pltpu.VMEM((1, 2, hb), jnp.int32),
            pltpu.VMEM((2, 1, 2, hb), jnp.int32),
            pltpu.VMEM((2 * hb, 8, LANES), jnp.int32),
            pltpu.SemaphoreType.DMA((dloc,)),
            pltpu.SemaphoreType.DMA((dloc,)),
            pltpu.SemaphoreType.DMA((7,)),
            pltpu.SemaphoreType.DMA((2,)),
            pltpu.SemaphoreType.DMA((2,)),
            pltpu.SemaphoreType.DMA((ITERS, 2, pairs)),
            pltpu.SemaphoreType.DMA((ITERS, 2, pairs)),
            pltpu.SemaphoreType.DMA((ITERS,)),
            pltpu.SemaphoreType.DMA((ITERS,)),
        ],
        compiler_params=pltpu.CompilerParams(
            collective_id=0, has_side_effects=True, vmem_limit_bytes=60 * 1024 * 1024
        ),
    )(
        field,
        group_speed,
        face_angle.reshape(fblk, LANES),
        face_speed.reshape(fblk, LANES),
        face_cells,
        face_live,
        halo_blocks,
        cell_level.reshape(1, own),
        polar_mask.reshape(1, own),
        turn_rate.reshape(1, own),
    )


def solution(mesh):
    return jax.shard_map(
        on_device,
        mesh=mesh,
        in_specs=(
            P("spec", None, "rows"),
            P(),
            P("rows"),
            P("rows"),
            P(None, "rows"),
            P("rows"),
            P("rows", None, None),
            P("rows"),
            P("rows"),
            P("rows"),
        ),
        out_specs=P("spec", None, "rows"),
        check_vma=False,
    )
```

time: 226 us -> 69.7 us (0.31)
  the two profiles are of different devices: /device:TPU:95 before, /device:TPU:64 now
where the time goes in v1:
time: 69.7 us; the launch traced here: 69.5 us
  Pallas kernels  66.4 us (95%)
  local copies, waits for them, and re-layouts  2.41 us (3%)
    pallas_call x1, Pallas kernels, on_device(): pl.pallas_call(kernel, out_shape=jax.ShapeDtypeStruct(field.shape, field....  66.4 us
    unnamed x1, local copies, waits for them, and re-layouts  2.41 us

profile of v1, /device:TPU:64, one launch (start us, length us, event | category | flops | bytes accessed | tf_op | source)
XLA Modules:
  0.0 69.5 jit_solution(14798657470889899327)
XLA Ops:
  0.7 66.4 %shard_map.100 = f32[18,30,512]{2,1,0:T(8,128)} custom-call(f32[18,30,512]{2,1,0:T(8,128)} %field.1, f32[30]{0:T(128)} %speed_s.1, f32[8,128]{1,0:T(8,128)} %bitcast.5, f32[8,128]{1,0:T(8,128)} %bitcast.6, s32[2,1024]{1,0:T(2,128)} %cells_h.1, s32[1]{0:T(128)S(6)} %copy.12.live_s, s32[1,2,2]{2,1,0:T(2,128)} %table_h.1, s32[1,512]{1,0:T(1,128)} %bitcast.7, ...), custom_call_target="tpu_custom_call" | custom-call | tf_op jit(solution)/shard_map/pallas_call | solution.py:435
  67.1 2.4 %copy.13 = f32[18,30,512]{2,1,0:T(8,128)} copy(f32[18,30,512]{2,1,0:T(8,128)} %shard_map.100) | data formatting | bytes 2211840

commit v2 on v1

--- a/solution.py
+++ b/solution.py
@@ -41,10 +41,8 @@
     got,
     edge_sent,
     edge_got,
-    ext_hi,
-    ext_lo,
-    flux_hi,
-    flux_lo,
+    ext,
+    flux,
     own_hot,
     up_hot,
     back_hot,
@@ -60,11 +58,13 @@
     table_v,
     table_r,
     picks,
+    full,
     load_sem,
-    out_sem,
     small_sem,
     table_send,
     table_recv,
+    full_send,
+    full_recv,
     send_sem,
     recv_sem,
     edge_send,
@@ -72,7 +72,7 @@
 ):
     dloc, nfreq, own = field.shape
     pairs = dloc // 2
-    chunks = pairs // CHUNK
+    span = 2 * CHUNK * ROWS
     hb = table_h.shape[2]
     faces = cells.shape[1]
     fblk = faces // LANES
@@ -142,6 +142,33 @@
         @pl.when(has[side])
         def _():
             tables[side].start()
+
+    def full_copy(side, p):
+        return pltpu.make_async_remote_copy(
+            src_ref=field.at[direction(p)],
+            dst_ref=full.at[1 - side, p],
+            send_sem=full_send.at[side, p],
+            recv_sem=full_recv.at[1 - side, p],
+            device_id=peer[side],
+            device_id_type=MESH,
+        )
+
+    def full_arrival(side, p):
+        return pltpu.make_async_remote_copy(
+            src_ref=field.at[direction(p)],
+            dst_ref=full.at[side, p],
+            send_sem=full_send.at[side, p],
+            recv_sem=full_recv.at[side, p],
+            device_id=peer[side],
+            device_id_type=MESH,
+        )
+
+    for side in (0, 1):
+
+        @pl.when(has[side])
+        def _():
+            for p in range(2 * CHUNK):
+                full_copy(side, p).start()
 
     for copy in small[1:]:
         copy.wait()
@@ -230,8 +257,15 @@
                 taken[1 - side : 2 - side, k : k + 1], (8, LANES)
             )
 
-    def pick(value, side, k):
-        wanted = jnp.broadcast_to(picks[side * hb + k, 0:1, :], (nfreq, LANES))
+    mine = table_v[0]
+    for side in (0, 1):
+        for k in range(hb):
+            picks[(2 + side) * hb + k] = jnp.broadcast_to(
+                mine[side : side + 1, k : k + 1], (8, LANES)
+            )
+
+    def pick(value, which):
+        wanted = jnp.broadcast_to(picks[which, 0:1, :], (nfreq, LANES))
         chosen = value[:, 0:LANES]
         for c in range(1, own // LANES):
             chosen = jnp.where(wanted == c, value[:, c * LANES : (c + 1) * LANES], chosen)
@@ -262,24 +296,36 @@
             for e in (0, 1):
                 value = cur[2 * pair + e]
                 for k in range(hb):
-                    sent[step, side, pair, e, k] = pick(value, side, k)
+                    sent[step, side, pair, e, k] = pick(value, side * hb + k)
 
             @pl.when(has[side])
             def _():
                 halo_copy(step, side, pair).start()
 
+    def put(p, at, value):
+        first = (p // (2 * CHUNK)) * 2 * span + (p % (2 * CHUNK)) * ROWS
+        high, low = split(value)
+        ext[first : first + nfreq, at] = high
+        ext[first + span : first + span + nfreq, at] = low
+
     def split_own(p):
-        rows = pl.ds(p * ROWS, nfreq)
-        high, low = split(cur[p])
-        ext_hi[rows, 0:own] = high
-        ext_lo[rows, 0:own] = low
-
-    for pair in range(pairs):
-        for e in (0, 1):
-            loads[2 * pair + e].wait()
+        put(p, slice(0, own), cur[p])
+
+    for copy in loads:
+        copy.wait()
+    for pair in range(CHUNK, pairs):
         send_pair(0, pair)
     for p in range(dloc):
         split_own(p)
+    for side in (0, 1):
+
+        @pl.when(has[side])
+        def _():
+            for p in range(2 * CHUNK):
+                full_arrival(side, p).wait_recv()
+                value = full[side, p]
+                for k in range(hb):
+                    got[0, side, p // 2, p % 2, k] = pick(value, (2 + side) * hb + k)
 
     def turn_slot(step, p):
         d = direction(p)
@@ -299,14 +345,6 @@
             device_id_type=MESH,
         )
 
-    def store_pair(pair):
-        return [
-            pltpu.make_async_copy(
-                cur.at[p], out.at[direction(p)], out_sem.at[p]
-            )
-            for p in (2 * pair, 2 * pair + 1)
-        ]
-
     def finish_pair(step, pair):
         turn_slot(step, 2 * pair)
         turn_slot(step, 2 * pair + 1)
@@ -317,37 +355,33 @@
 
         @pl.when(step == ITERS - 1)
         def _():
-            for copy in store_pair(pair):
-                copy.start()
+            for p in (2 * pair, 2 * pair + 1):
+                out[direction(p)] = cur[p]
 
     def compute(step, chunk):
-        span = 2 * CHUNK * ROWS
-        rows = pl.ds(chunk * span, span)
+        rows = slice(chunk * 2 * span, (chunk + 1) * 2 * span)
         for i in range(CHUNK):
             pair = chunk * CHUNK + i
             for side in (0, 1):
 
-                @pl.when(has[side])
+                awaited = has[side] if chunk > 0 else has[side] & (step > 0)
+
+                @pl.when(awaited)
                 def _():
                     halo_arrival(step, side, pair).wait_recv()
 
             for side in (0, 1):
                 for e in (0, 1):
                     for k in range(hb):
-                        high, low = split(got[step, side, pair, e, k])
-                        at = pl.ds(own + (side * hb + k) * LANES, LANES)
-                        there = pl.ds((2 * pair + e) * ROWS, nfreq)
-                        ext_hi[there, at] = high
-                        ext_lo[there, at] = low
+                        first = own + (side * hb + k) * LANES
+                        put(2 * pair + e, slice(first, first + LANES), got[step, side, pair, e, k])
         width = 2 * LANES
         for n in range(faces // width):
             at = slice(n * width, (n + 1) * width)
-            low = jnp.dot(
-                ext_hi[rows, 0:own], own_hot[:, at], preferred_element_type=F32
-            ) + jnp.dot(ext_lo[rows, 0:own], own_hot[:, at], preferred_element_type=F32)
-            upp = jnp.dot(
-                ext_hi[rows, :], up_hot[:, at], preferred_element_type=F32
-            ) + jnp.dot(ext_lo[rows, :], up_hot[:, at], preferred_element_type=F32)
+            low = jnp.dot(ext[rows, 0:own], own_hot[:, at], preferred_element_type=F32)
+            upp = jnp.dot(ext[rows, :], up_hot[:, at], preferred_element_type=F32)
+            low = low[0:span] + low[span : 2 * span]
+            upp = upp[0:span] + upp[span : 2 * span]
             for i in range(2 * CHUNK):
                 p = chunk * 2 * CHUNK + i
                 there = slice(i * ROWS, (i + 1) * ROWS)
@@ -359,11 +393,10 @@
                     flow = u * jnp.where(u > 0.0, low[there, inner], upp[there, inner])
                     high, rest = split(flow)
                     outer = slice(n * width + h * LANES, n * width + (h + 1) * LANES)
-                    flux_hi[there, outer] = high
-                    flux_lo[there, outer] = rest
-        total = jnp.dot(flux_hi[...], back_hot[...], preferred_element_type=F32) + jnp.dot(
-            flux_lo[...], back_hot[...], preferred_element_type=F32
-        )
+                    flux[there, outer] = high
+                    flux[slice(span + i * ROWS, span + (i + 1) * ROWS), outer] = rest
+        total = jnp.dot(flux[...], back_hot[...], preferred_element_type=F32)
+        total = total[0:span] + total[span : 2 * span]
         for i in range(2 * CHUNK):
             p = chunk * 2 * CHUNK + i
             moved[p] = cur[p] - scale[...] * total[i * ROWS : i * ROWS + nfreq]
@@ -384,30 +417,18 @@
 
     lax.fori_loop(0, ITERS, one_step, 0)
 
+    for step in range(ITERS):
+        edge_copy(step).wait_send()
     for side in (0, 1):
 
         @pl.when(has[side])
         def _():
             tables[side].wait_send()
-
-    def drain(step, carry):
-        edge_copy(step).wait_send()
-        for side in (0, 1):
-
-            @pl.when(has[side])
-            def _():
-                def inner(pair, c):
+            for p in range(2 * CHUNK):
+                full_copy(side, p).wait_send()
+            for step in range(ITERS):
+                for pair in range(CHUNK if step == 0 else 0, pairs):
                     halo_copy(step, side, pair).wait_send()
-                    return c
-
-                lax.fori_loop(0, pairs, inner, 0)
-
-        return carry
-
-    lax.fori_loop(0, ITERS, drain, 0)
-    for pair in range(pairs):
-        for copy in store_pair(pair):
-            copy.wait()
 
 
 def on_device(
@@ -434,7 +455,7 @@
     span = 2 * CHUNK * ROWS
     return pl.pallas_call(
         kernel,
-        out_shape=jax.ShapeDtypeStruct(field.shape, field.dtype),
+        out_shape=pltpu.VMEM(field.shape, field.dtype),
         in_specs=[
             any_spec,
             smem_spec,
@@ -447,7 +468,7 @@
             any_spec,
             any_spec,
         ],
-        out_specs=any_spec,
+        out_specs=pl.BlockSpec(memory_space=pltpu.VMEM),
         scratch_shapes=[
             pltpu.VMEM((dloc, nfreq, own), F32),
             pltpu.VMEM((dloc, nfreq, own), F32),
@@ -455,10 +476,8 @@
             pltpu.VMEM(halo, F32),
             pltpu.VMEM((ITERS, 2, nfreq, own), F32),
             pltpu.VMEM((ITERS, 2, nfreq, own), F32),
-            pltpu.VMEM((dloc * ROWS, ext), BF16),
-            pltpu.VMEM((dloc * ROWS, ext), BF16),
-            pltpu.VMEM((span, faces), BF16),
-            pltpu.VMEM((span, faces), BF16),
+            pltpu.VMEM((2 * dloc * ROWS, ext), BF16),
+            pltpu.VMEM((2 * span, faces), BF16),
             pltpu.VMEM((own, faces), BF16),
             pltpu.VMEM((ext, faces), BF16),
             pltpu.VMEM((faces, own), BF16),
@@ -473,12 +492,14 @@
             pltpu.VMEM((1, own), F32),
             pltpu.VMEM((1, 2, hb), jnp.int32),
             pltpu.VMEM((2, 1, 2, hb), jnp.int32),
-            pltpu.VMEM((2 * hb, 8, LANES), jnp.int32),
-            pltpu.SemaphoreType.DMA((dloc,)),
+            pltpu.VMEM((4 * hb, 8, LANES), jnp.int32),
+            pltpu.VMEM((2, 2 * CHUNK, nfreq, own), F32),
             pltpu.SemaphoreType.DMA((dloc,)),
             pltpu.SemaphoreType.DMA((7,)),
             pltpu.SemaphoreType.DMA((2,)),
             pltpu.SemaphoreType.DMA((2,)),
+            pltpu.SemaphoreType.DMA((2, 2 * CHUNK)),
+            pltpu.SemaphoreType.DMA((2, 2 * CHUNK)),
             pltpu.SemaphoreType.DMA((ITERS, 2, pairs)),
             pltpu.SemaphoreType.DMA((ITERS, 2, pairs)),
             pltpu.SemaphoreType.DMA((ITERS,)),

time: 69.7 us -> 65 us (0.933)
  the two profiles are of different devices: /device:TPU:64 before, /device:TPU:192 now
where the time goes in v2:
time: 65 us; the launch traced here: 64.6 us
  Pallas kernels  62.9 us (97%)
  local copies, waits for them, and re-layouts  1.02 us (2%)
  between operations  0.66 us (1%)
    pallas_call x1, Pallas kernels, on_device(): pl.pallas_call(kernel, out_shape=pltpu.VMEM(field.shape, field.dtype), in...  62.9 us

profile of v2, /device:TPU:192, one launch (start us, length us, event | category | flops | bytes accessed | tf_op | source)
XLA Modules:
  0.0 64.6 jit_solution(11112367331715668433)
XLA Ops:
  0.7 62.9 %shard_map.100 = f32[18,30,512]{2,1,0:T(8,128)S(1)} custom-call(f32[18,30,512]{2,1,0:T(8,128)} %field.1, f32[30]{0:T(128)} %speed_s.1, f32[8,128]{1,0:T(8,128)} %bitcast.5, f32[8,128]{1,0:T(8,128)} %bitcast.6, s32[2,1024]{1,0:T(2,128)} %cells_h.1, s32[1]{0:T(128)S(6)} %copy.13.live_s, s32[1,2,2]{2,1,0:T(2,128)} %table_h.1, s32[1,512]{1,0:T(1,128)} %bitcast.7, ...), custom_call_target="tpu_custom_call" | custom-call | tf_op jit(solution)/shard_map/pallas_call | solution.py:456
  63.6 1.0 %copy.12 = f32[18,30,512]{2,1,0:T(8,128)} copy(f32[18,30,512]{2,1,0:T(8,128)S(1)} %shard_map.100) | data formatting | bytes 2211840

commit v3 on v2

--- a/solution.py
+++ b/solution.py
@@ -13,7 +13,10 @@
 ITERS = 3
 LANES = 128
 ROWS = 32
-CHUNK = 3
+CHUNKS = ((0, 2), (2, 2), (4, 2), (6, 2), (8, 1))
+AHEAD = 2
+EDGE_AT = 2
+HOT = jnp.float8_e4m3fn
 BF16 = jnp.bfloat16
 F32 = jnp.float32
 
@@ -72,7 +75,6 @@
 ):
     dloc, nfreq, own = field.shape
     pairs = dloc // 2
-    span = 2 * CHUNK * ROWS
     hb = table_h.shape[2]
     faces = cells.shape[1]
     fblk = faces // LANES
@@ -167,7 +169,7 @@
 
         @pl.when(has[side])
         def _():
-            for p in range(2 * CHUNK):
+            for p in range(2 * AHEAD):
                 full_copy(side, p).start()
 
     for copy in small[1:]:
@@ -185,18 +187,18 @@
         for c in range(own // LANES):
             own_hot[c * LANES : (c + 1) * LANES, at] = jnp.where(
                 low == sub + c * LANES, one, zero
-            ).astype(BF16)
+            ).astype(HOT)
         for c in range(up_hot.shape[0] // LANES):
             up_hot[c * LANES : (c + 1) * LANES, at] = jnp.where(
                 upp == sub + c * LANES, one, zero
-            ).astype(BF16)
+            ).astype(HOT)
         low_t = low.T
         upp_t = upp.T
         for c in range(own // LANES):
             here = lane + c * LANES
             back_hot[at, c * LANES : (c + 1) * LANES] = (
                 jnp.where(low_t == here, one, zero) - jnp.where(upp_t == here, one, zero)
-            ).astype(BF16)
+            ).astype(HOT)
         return carry
 
     lax.fori_loop(0, fblk, build, 0)
@@ -302,8 +304,13 @@
             def _():
                 halo_copy(step, side, pair).start()
 
+    home = {}
+    for begin, count in CHUNKS:
+        for p in range(2 * begin, 2 * (begin + count)):
+            home[p] = (4 * begin * ROWS + (p - 2 * begin) * ROWS, 2 * count * ROWS)
+
     def put(p, at, value):
-        first = (p // (2 * CHUNK)) * 2 * span + (p % (2 * CHUNK)) * ROWS
+        first, span = home[p]
         high, low = split(value)
         ext[first : first + nfreq, at] = high
         ext[first + span : first + span + nfreq, at] = low
@@ -313,7 +320,7 @@
 
     for copy in loads:
         copy.wait()
-    for pair in range(CHUNK, pairs):
+    for pair in range(AHEAD, pairs):
         send_pair(0, pair)
     for p in range(dloc):
         split_own(p)
@@ -321,7 +328,7 @@
 
         @pl.when(has[side])
         def _():
-            for p in range(2 * CHUNK):
+            for p in range(2 * AHEAD):
                 full_arrival(side, p).wait_recv()
                 value = full[side, p]
                 for k in range(hb):
@@ -359,12 +366,12 @@
                 out[direction(p)] = cur[p]
 
     def compute(step, chunk):
-        rows = slice(chunk * 2 * span, (chunk + 1) * 2 * span)
-        for i in range(CHUNK):
-            pair = chunk * CHUNK + i
+        begin, count = CHUNKS[chunk]
+        span = 2 * count * ROWS
+        rows = slice(4 * begin * ROWS, 4 * begin * ROWS + 2 * span)
+        for pair in range(begin, begin + count):
             for side in (0, 1):
-
-                awaited = has[side] if chunk > 0 else has[side] & (step > 0)
+                awaited = has[side] if pair >= AHEAD else has[side] & (step > 0)
 
                 @pl.when(awaited)
                 def _():
@@ -382,8 +389,8 @@
             upp = jnp.dot(ext[rows, :], up_hot[:, at], preferred_element_type=F32)
             low = low[0:span] + low[span : 2 * span]
             upp = upp[0:span] + upp[span : 2 * span]
-            for i in range(2 * CHUNK):
-                p = chunk * 2 * CHUNK + i
+            for i in range(2 * count):
+                p = 2 * begin + i
                 there = slice(i * ROWS, (i + 1) * ROWS)
                 for h in range(2):
                     inner = slice(h * LANES, (h + 1) * LANES)
@@ -395,24 +402,27 @@
                     outer = slice(n * width + h * LANES, n * width + (h + 1) * LANES)
                     flux[there, outer] = high
                     flux[slice(span + i * ROWS, span + (i + 1) * ROWS), outer] = rest
-        total = jnp.dot(flux[...], back_hot[...], preferred_element_type=F32)
+        total = jnp.dot(flux[0 : 2 * span, :], back_hot[...], preferred_element_type=F32)
         total = total[0:span] + total[span : 2 * span]
-        for i in range(2 * CHUNK):
-            p = chunk * 2 * CHUNK + i
+        for i in range(2 * count):
+            p = 2 * begin + i
             moved[p] = cur[p] - scale[...] * total[i * ROWS : i * ROWS + nfreq]
 
     def one_step(step, carry):
-        compute(step, 0)
-        edge_sent[step] = moved[0:2]
-        edge_copy(step).start()
-        finish_pair(step, 1)
-        compute(step, 1)
-        edge_copy(step).wait_recv()
-        for pair in (0, 2, 3, 4):
-            finish_pair(step, pair)
-        compute(step, 2)
-        for pair in (5, 6, 7, 8):
-            finish_pair(step, pair)
+        done = 1
+        for chunk, (begin, count) in enumerate(CHUNKS):
+            compute(step, chunk)
+            if chunk == 0:
+                edge_sent[step] = moved[0:2]
+                edge_copy(step).start()
+            if chunk == EDGE_AT:
+                edge_copy(step).wait_recv()
+                finish_pair(step, 0)
+            last = begin + count == pairs
+            ready = pairs if last else begin + count - 1
+            for pair in range(done, ready):
+                finish_pair(step, pair)
+            done = max(done, ready)
         return carry
 
     lax.fori_loop(0, ITERS, one_step, 0)
@@ -424,10 +434,10 @@
         @pl.when(has[side])
         def _():
             tables[side].wait_send()
-            for p in range(2 * CHUNK):
+            for p in range(2 * AHEAD):
                 full_copy(side, p).wait_send()
             for step in range(ITERS):
-                for pair in range(CHUNK if step == 0 else 0, pairs):
+                for pair in range(AHEAD if step == 0 else 0, pairs):
                     halo_copy(step, side, pair).wait_send()
 
 
@@ -452,7 +462,7 @@
     any_spec = pl.BlockSpec(memory_space=pl.ANY)
     smem_spec = pl.BlockSpec(memory_space=pltpu.SMEM)
     halo = (ITERS, 2, pairs, 2, hb, nfreq, LANES)
-    span = 2 * CHUNK * ROWS
+    span = 2 * max(count for _, count in CHUNKS) * ROWS
     return pl.pallas_call(
         kernel,
         out_shape=pltpu.VMEM(field.shape, field.dtype),
@@ -478,9 +488,9 @@
             pltpu.VMEM((ITERS, 2, nfreq, own), F32),
             pltpu.VMEM((2 * dloc * ROWS, ext), BF16),
             pltpu.VMEM((2 * span, faces), BF16),
-            pltpu.VMEM((own, faces), BF16),
-            pltpu.VMEM((ext, faces), BF16),
-            pltpu.VMEM((faces, own), BF16),
+            pltpu.VMEM((own, faces), HOT),
+            pltpu.VMEM((ext, faces), HOT),
+            pltpu.VMEM((faces, own), HOT),
             pltpu.VMEM((dloc, fblk, LANES), F32),
             pltpu.VMEM((nfreq, own), F32),
             pltpu.VMEM((2, own), F32),
@@ -493,13 +503,13 @@
             pltpu.VMEM((1, 2, hb), jnp.int32),
             pltpu.VMEM((2, 1, 2, hb), jnp.int32),
             pltpu.VMEM((4 * hb, 8, LANES), jnp.int32),
-            pltpu.VMEM((2, 2 * CHUNK, nfreq, own), F32),
+            pltpu.VMEM((2, 2 * AHEAD, nfreq, own), F32),
             pltpu.SemaphoreType.DMA((dloc,)),
             pltpu.SemaphoreType.DMA((7,)),
             pltpu.SemaphoreType.DMA((2,)),
             pltpu.SemaphoreType.DMA((2,)),
-            pltpu.SemaphoreType.DMA((2, 2 * CHUNK)),
-            pltpu.SemaphoreType.DMA((2, 2 * CHUNK)),
+            pltpu.SemaphoreType.DMA((2, 2 * AHEAD)),
+            pltpu.SemaphoreType.DMA((2, 2 * AHEAD)),
             pltpu.SemaphoreType.DMA((ITERS, 2, pairs)),
             pltpu.SemaphoreType.DMA((ITERS, 2, pairs)),
             pltpu.SemaphoreType.DMA((ITERS,)),

time: 65 us -> 63.2 us (0.972)
  the two profiles are of different devices: /device:TPU:192 before, /device:TPU:160 now
where the time goes in v3:
time: 63.2 us; the launch traced here: 63.1 us
  Pallas kernels  61.4 us (97%)
  local copies, waits for them, and re-layouts  1.02 us (2%)
  between operations  0.66 us (1%)
    pallas_call x1, Pallas kernels, on_device(): pl.pallas_call(kernel, out_shape=pltpu.VMEM(field.shape, field.dtype), in...  61.4 us

profile of v3, /device:TPU:160, one launch (start us, length us, event | category | flops | bytes accessed | tf_op | source)
XLA Modules:
  0.0 63.1 jit_solution(2233103259691824110)
XLA Ops:
  0.7 61.4 %shard_map.100 = f32[18,30,512]{2,1,0:T(8,128)S(1)} custom-call(f32[18,30,512]{2,1,0:T(8,128)} %field.1, f32[30]{0:T(128)} %speed_s.1, f32[8,128]{1,0:T(8,128)} %bitcast.5, f32[8,128]{1,0:T(8,128)} %bitcast.6, s32[2,1024]{1,0:T(2,128)} %cells_h.1, s32[1]{0:T(128)S(6)} %copy.13.live_s, s32[1,2,2]{2,1,0:T(2,128)} %table_h.1, s32[1,512]{1,0:T(1,128)} %bitcast.7, ...), custom_call_target="tpu_custom_call" | custom-call | tf_op jit(solution)/shard_map/pallas_call | solution.py:466
  62.1 1.0 %copy.12 = f32[18,30,512]{2,1,0:T(8,128)} copy(f32[18,30,512]{2,1,0:T(8,128)S(1)} %shard_map.100) | data formatting | bytes 2211840

commit v4 on v3

--- a/solution.py
+++ b/solution.py
@@ -16,6 +16,8 @@
 CHUNKS = ((0, 2), (2, 2), (4, 2), (6, 2), (8, 1))
 AHEAD = 2
 EDGE_AT = 2
+PLANE = 32
+UP, DOWN = 7, 25
 HOT = jnp.float8_e4m3fn
 BF16 = jnp.bfloat16
 F32 = jnp.float32
@@ -62,12 +64,15 @@
     table_r,
     picks,
     full,
+    passing,
     load_sem,
     small_sem,
     table_send,
     table_recv,
     full_send,
     full_recv,
+    pass_send,
+    pass_recv,
     send_sem,
     recv_sem,
     edge_send,
@@ -85,6 +90,23 @@
     peer = ({"rows": jnp.maximum(row - 1, 0)}, {"rows": jnp.minimum(row + 1, size - 1)})
     partner = {"spec": 1 - spec}
 
+    at = lax.rem(row, PLANE)
+    odd = spec == 1
+
+    def other(shift):
+        return {"rows": jnp.clip(row + shift, 0, size - 1)}
+
+    via = (odd & (at == 0) & (row > 0), odd & (at == PLANE - 1) & (row < size - 1))
+    passes_up = odd & (at == UP) & (row < size - PLANE)
+    passes_down = odd & (at == DOWN) & (row >= PLANE)
+    relay = (other(DOWN), other(UP + 1 - PLANE))
+    roles = (
+        (via[0], relay[0], other(UP - PLANE)),
+        (via[1], relay[1], other(DOWN + 1)),
+        (passes_up, other(PLANE - 1 - UP), other(PLANE - UP)),
+        (passes_down, other(-DOWN), other(-DOWN - 1)),
+    )
+
     def slot(d):
         return 2 * d if d < pairs else 2 * (dloc - 1 - d) + 1
 
@@ -125,7 +147,16 @@
         def _():
             pl.semaphore_signal(barrier, inc=1, device_id=peer[side], device_id_type=MESH)
 
-    pl.semaphore_wait(barrier, 1 + has[0].astype(jnp.int32) + has[1].astype(jnp.int32))
+    peers = 1 + has[0].astype(jnp.int32) + has[1].astype(jnp.int32)
+    for role, first, second in roles:
+
+        @pl.when(role)
+        def _():
+            pl.semaphore_signal(barrier, inc=1, device_id=first, device_id_type=MESH)
+            pl.semaphore_signal(barrier, inc=1, device_id=second, device_id_type=MESH)
+
+        peers = peers + 2 * role.astype(jnp.int32)
+    pl.semaphore_wait(barrier, peers)
 
     small[0].wait()
     tables = [
@@ -283,6 +314,45 @@
             device_id_type=MESH,
         )
 
+    def via_copy(step, side, pair):
+        return pltpu.make_async_remote_copy(
+            src_ref=sent.at[step, side, pair],
+            dst_ref=passing.at[step, pair],
+            send_sem=send_sem.at[step, side, pair],
+            recv_sem=pass_recv.at[step, pair],
+            device_id=relay[side],
+            device_id_type=MESH,
+        )
+
+    def pass_copy(step, side, pair):
+        return pltpu.make_async_remote_copy(
+            src_ref=passing.at[step, pair],
+            dst_ref=got.at[step, 1 - side, pair],
+            send_sem=pass_send.at[step, pair],
+            recv_sem=recv_sem.at[step, 1 - side, pair],
+            device_id=other(-DOWN - 1) if side == 0 else other(PLANE - UP),
+            device_id_type=MESH,
+        )
+
+    def pass_on(step, first):
+        for side, role in ((0, passes_down), (1, passes_up)):
+
+            @pl.when(role)
+            def _():
+                def one(pair, carry):
+                    pltpu.make_async_remote_copy(
+                        src_ref=passing.at[step, pair],
+                        dst_ref=passing.at[step, pair],
+                        send_sem=pass_send.at[step, pair],
+                        recv_sem=pass_recv.at[step, pair],
+                        device_id=other(1),
+                        device_id_type=MESH,
+                    ).wait_recv()
+                    pass_copy(step, side, pair).start()
+                    return carry
+
+                lax.fori_loop(first, pairs, one, 0)
+
     def halo_arrival(step, side, pair):
         return pltpu.make_async_remote_copy(
             src_ref=sent.at[step, side, pair],
@@ -300,9 +370,13 @@
                 for k in range(hb):
                     sent[step, side, pair, e, k] = pick(value, side * hb + k)
 
-            @pl.when(has[side])
+            @pl.when(has[side] & jnp.logical_not(via[side]))
             def _():
                 halo_copy(step, side, pair).start()
+
+            @pl.when(via[side])
+            def _():
+                via_copy(step, side, pair).start()
 
     home = {}
     for begin, count in CHUNKS:
@@ -324,6 +398,7 @@
         send_pair(0, pair)
     for p in range(dloc):
         split_own(p)
+    pass_on(0, AHEAD)
     for side in (0, 1):
 
         @pl.when(has[side])
@@ -409,6 +484,10 @@
             moved[p] = cur[p] - scale[...] * total[i * ROWS : i * ROWS + nfreq]
 
     def one_step(step, carry):
+        @pl.when(step > 0)
+        def _():
+            pass_on(step, 0)
+
         done = 1
         for chunk, (begin, count) in enumerate(CHUNKS):
             compute(step, chunk)
@@ -429,6 +508,14 @@
 
     for step in range(ITERS):
         edge_copy(step).wait_send()
+    for side, role in ((0, passes_down), (1, passes_up)):
+
+        @pl.when(role)
+        def _():
+            for step in range(ITERS):
+                for pair in range(AHEAD if step == 0 else 0, pairs):
+                    pass_copy(step, side, pair).wait_send()
+
     for side in (0, 1):
 
         @pl.when(has[side])
@@ -504,12 +591,15 @@
             pltpu.VMEM((2, 1, 2, hb), jnp.int32),
             pltpu.VMEM((4 * hb, 8, LANES), jnp.int32),
             pltpu.VMEM((2, 2 * AHEAD, nfreq, own), F32),
+            pltpu.VMEM((ITERS, pairs, 2, hb, nfreq, LANES), F32),
             pltpu.SemaphoreType.DMA((dloc,)),
             pltpu.SemaphoreType.DMA((7,)),
             pltpu.SemaphoreType.DMA((2,)),
             pltpu.SemaphoreType.DMA((2,)),
             pltpu.SemaphoreType.DMA((2, 2 * AHEAD)),
             pltpu.SemaphoreType.DMA((2, 2 * AHEAD)),
+            pltpu.SemaphoreType.DMA((ITERS, pairs)),
+            pltpu.SemaphoreType.DMA((ITERS, pairs)),
             pltpu.SemaphoreType.DMA((ITERS, 2, pairs)),
             pltpu.SemaphoreType.DMA((ITERS, 2, pairs)),
             pltpu.SemaphoreType.DMA((ITERS,)),

time: 63.2 us -> 56.9 us (0.900)
  the two profiles are of different devices: /device:TPU:160 before, /device:TPU:64 now
where the time goes in v4:
time: 56.9 us; the launch traced here: 56.7 us
  Pallas kernels  55 us (97%)
  local copies, waits for them, and re-layouts  1.02 us (2%)
  between operations  0.66 us (1%)
    pallas_call x1, Pallas kernels, on_device(): pl.pallas_call(kernel, out_shape=pltpu.VMEM(field.shape, field.dtype), in...  55 us

profile of v4, /device:TPU:64, one launch (start us, length us, event | category | flops | bytes accessed | tf_op | source)
XLA Modules:
  0.0 56.7 jit_solution(504839813820840747)
XLA Ops:
  0.7 55.0 %shard_map.100 = f32[18,30,512]{2,1,0:T(8,128)S(1)} custom-call(f32[18,30,512]{2,1,0:T(8,128)} %field.1, f32[30]{0:T(128)} %speed_s.1, f32[8,128]{1,0:T(8,128)} %bitcast.5, f32[8,128]{1,0:T(8,128)} %bitcast.6, s32[2,1024]{1,0:T(2,128)} %cells_h.1, s32[1]{0:T(128)S(6)} %copy.13.live_s, s32[1,2,2]{2,1,0:T(2,128)} %table_h.1, s32[1,512]{1,0:T(1,128)} %bitcast.7, ...), custom_call_target="tpu_custom_call" | custom-call | tf_op jit(solution)/shard_map/pallas_call | solution.py:553
  55.7 1.0 %copy.12 = f32[18,30,512]{2,1,0:T(8,128)} copy(f32[18,30,512]{2,1,0:T(8,128)S(1)} %shard_map.100) | data formatting | bytes 2211840

commit v5 on v4

--- a/solution.py
+++ b/solution.py
@@ -14,6 +14,7 @@
 LANES = 128
 ROWS = 32
 CHUNKS = ((0, 2), (2, 2), (4, 2), (6, 2), (8, 1))
+GROUPS = ((0, 1), (2, 3, 4))
 AHEAD = 2
 EDGE_AT = 2
 PLANE = 32
@@ -48,6 +49,8 @@
     edge_got,
     ext,
     flux,
+    pre_low,
+    pre_upp,
     own_hot,
     up_hot,
     back_hot,
@@ -176,9 +179,12 @@
         def _():
             tables[side].start()
 
+    for copy in loads[0 : 2 * AHEAD]:
+        copy.wait()
+
     def full_copy(side, p):
         return pltpu.make_async_remote_copy(
-            src_ref=field.at[direction(p)],
+            src_ref=cur.at[p],
             dst_ref=full.at[1 - side, p],
             send_sem=full_send.at[side, p],
             recv_sem=full_recv.at[1 - side, p],
@@ -188,7 +194,7 @@
 
     def full_arrival(side, p):
         return pltpu.make_async_remote_copy(
-            src_ref=field.at[direction(p)],
+            src_ref=cur.at[p],
             dst_ref=full.at[side, p],
             send_sem=full_send.at[side, p],
             recv_sem=full_recv.at[side, p],
@@ -392,22 +398,29 @@
     def split_own(p):
         put(p, slice(0, own), cur[p])
 
-    for copy in loads:
+    for copy in loads[2 * AHEAD :]:
         copy.wait()
     for pair in range(AHEAD, pairs):
         send_pair(0, pair)
     for p in range(dloc):
         split_own(p)
-    pass_on(0, AHEAD)
-    for side in (0, 1):
-
-        @pl.when(has[side])
-        def _():
-            for p in range(2 * AHEAD):
-                full_arrival(side, p).wait_recv()
-                value = full[side, p]
-                for k in range(hb):
-                    got[0, side, p // 2, p % 2, k] = pick(value, (2 + side) * hb + k)
+    def first_arrivals():
+        pass_on(0, AHEAD)
+        for side in (0, 1):
+
+            @pl.when(has[side])
+            def _():
+                for p in range(2 * AHEAD):
+                    full_arrival(side, p).wait_recv()
+                    value = full[side, p]
+                    for k in range(hb):
+                        got[0, side, p // 2, p % 2, k] = pick(value, (2 + side) * hb + k)
+        for side in (0, 1):
+
+            @pl.when(has[side])
+            def _():
+                for p in range(2 * AHEAD):
+                    full_copy(side, p).wait_send()
 
     def turn_slot(step, p):
         d = direction(p)
@@ -439,6 +452,23 @@
         def _():
             for p in (2 * pair, 2 * pair + 1):
                 out[direction(p)] = cur[p]
+
+    def prepare():
+        width = 2 * LANES
+        for group in GROUPS:
+            start = 4 * CHUNKS[group[0]][0] * ROWS
+            stop = 4 * sum(CHUNKS[group[-1]]) * ROWS
+            for n in range(faces // width):
+                at = slice(n * width, (n + 1) * width)
+                for hot, kept in ((own_hot[:, at], pre_low), (up_hot[0:own, at], pre_upp)):
+                    both = jnp.dot(ext[start:stop, 0:own], hot, preferred_element_type=F32)
+                    for chunk in group:
+                        begin, count = CHUNKS[chunk]
+                        span = 2 * count * ROWS
+                        here = 4 * begin * ROWS - start
+                        kept[2 * begin * ROWS : 2 * begin * ROWS + span, at] = (
+                            both[here : here + span] + both[here + span : here + 2 * span]
+                        )
 
     def compute(step, chunk):
         begin, count = CHUNKS[chunk]
@@ -460,10 +490,10 @@
         width = 2 * LANES
         for n in range(faces // width):
             at = slice(n * width, (n + 1) * width)
-            low = jnp.dot(ext[rows, 0:own], own_hot[:, at], preferred_element_type=F32)
-            upp = jnp.dot(ext[rows, :], up_hot[:, at], preferred_element_type=F32)
-            low = low[0:span] + low[span : 2 * span]
-            upp = upp[0:span] + upp[span : 2 * span]
+            upp = jnp.dot(ext[rows, own:], up_hot[own:, at], preferred_element_type=F32)
+            kept = slice(2 * begin * ROWS, 2 * begin * ROWS + span)
+            low = pre_low[kept, at]
+            upp = upp[0:span] + upp[span : 2 * span] + pre_upp[kept, at]
             for i in range(2 * count):
                 p = 2 * begin + i
                 there = slice(i * ROWS, (i + 1) * ROWS)
@@ -484,9 +514,15 @@
             moved[p] = cur[p] - scale[...] * total[i * ROWS : i * ROWS + nfreq]
 
     def one_step(step, carry):
+        prepare()
+
         @pl.when(step > 0)
         def _():
             pass_on(step, 0)
+
+        @pl.when(step == 0)
+        def _():
+            first_arrivals()
 
         done = 1
         for chunk, (begin, count) in enumerate(CHUNKS):
@@ -521,8 +557,6 @@
         @pl.when(has[side])
         def _():
             tables[side].wait_send()
-            for p in range(2 * AHEAD):
-                full_copy(side, p).wait_send()
             for step in range(ITERS):
                 for pair in range(AHEAD if step == 0 else 0, pairs):
                     halo_copy(step, side, pair).wait_send()
@@ -575,6 +609,8 @@
             pltpu.VMEM((ITERS, 2, nfreq, own), F32),
             pltpu.VMEM((2 * dloc * ROWS, ext), BF16),
             pltpu.VMEM((2 * span, faces), BF16),
+            pltpu.VMEM((dloc * ROWS, faces), F32),
+            pltpu.VMEM((dloc * ROWS, faces), F32),
             pltpu.VMEM((own, faces), HOT),
             pltpu.VMEM((ext, faces), HOT),
             pltpu.VMEM((faces, own), HOT),

time: 56.9 us -> 58.4 us (1.026)
  the two profiles are of different devices: /device:TPU:64 before, /device:TPU:192 now
where the time goes in v5:
time: 58.4 us; the launch traced here: 58.3 us
  Pallas kernels  56.6 us (97%)
  local copies, waits for them, and re-layouts  1.02 us (2%)
  between operations  0.66 us (1%)
    pallas_call x1, Pallas kernels, on_device(): pl.pallas_call(kernel, out_shape=pltpu.VMEM(field.shape, field.dtype), in...  56.6 us

profile of v5, /device:TPU:192, one launch (start us, length us, event | category | flops | bytes accessed | tf_op | source)
XLA Modules:
  0.0 58.3 jit_solution(4921230897972243775)
XLA Ops:
  0.7 56.6 %shard_map.100 = f32[18,30,512]{2,1,0:T(8,128)S(1)} custom-call(f32[18,30,512]{2,1,0:T(8,128)} %field.1, f32[30]{0:T(128)} %speed_s.1, f32[8,128]{1,0:T(8,128)} %bitcast.5, f32[8,128]{1,0:T(8,128)} %bitcast.6, s32[2,1024]{1,0:T(2,128)} %cells_h.1, s32[1]{0:T(128)S(6)} %copy.13.live_s, s32[1,2,2]{2,1,0:T(2,128)} %table_h.1, s32[1,512]{1,0:T(1,128)} %bitcast.7, ...), custom_call_target="tpu_custom_call" | custom-call | tf_op jit(solution)/shard_map/pallas_call | solution.py:587
  57.3 1.0 %copy.12 = f32[18,30,512]{2,1,0:T(8,128)} copy(f32[18,30,512]{2,1,0:T(8,128)S(1)} %shard_map.100) | data formatting | bytes 2211840

commit v6 on v4

--- a/solution.py
+++ b/solution.py
@@ -13,7 +13,7 @@
 ITERS = 3
 LANES = 128
 ROWS = 32
-CHUNKS = ((0, 2), (2, 2), (4, 2), (6, 2), (8, 1))
+CHUNKS = ((0, 1), (1, 2), (3, 2), (5, 2), (7, 1), (8, 1))
 AHEAD = 2
 EDGE_AT = 2
 PLANE = 32
@@ -176,9 +176,12 @@
         def _():
             tables[side].start()
 
+    for copy in loads[0 : 2 * AHEAD]:
+        copy.wait()
+
     def full_copy(side, p):
         return pltpu.make_async_remote_copy(
-            src_ref=field.at[direction(p)],
+            src_ref=cur.at[p],
             dst_ref=full.at[1 - side, p],
             send_sem=full_send.at[side, p],
             recv_sem=full_recv.at[1 - side, p],
@@ -188,7 +191,7 @@
 
     def full_arrival(side, p):
         return pltpu.make_async_remote_copy(
-            src_ref=field.at[direction(p)],
+            src_ref=cur.at[p],
             dst_ref=full.at[side, p],
             send_sem=full_send.at[side, p],
             recv_sem=full_recv.at[side, p],
@@ -392,7 +395,7 @@
     def split_own(p):
         put(p, slice(0, own), cur[p])
 
-    for copy in loads:
+    for copy in loads[2 * AHEAD :]:
         copy.wait()
     for pair in range(AHEAD, pairs):
         send_pair(0, pair)
@@ -408,6 +411,8 @@
                 value = full[side, p]
                 for k in range(hb):
                     got[0, side, p // 2, p % 2, k] = pick(value, (2 + side) * hb + k)
+            for p in range(2 * AHEAD):
+                full_copy(side, p).wait_send()
 
     def turn_slot(step, p):
         d = direction(p)
@@ -521,8 +526,6 @@
         @pl.when(has[side])
         def _():
             tables[side].wait_send()
-            for p in range(2 * AHEAD):
-                full_copy(side, p).wait_send()
             for step in range(ITERS):
                 for pair in range(AHEAD if step == 0 else 0, pairs):
                     halo_copy(step, side, pair).wait_send()

time: 56.9 us -> 55.6 us (0.977)
  the two profiles are of different devices: /device:TPU:64 before, /device:TPU:192 now
where the time goes in v6:
time: 55.6 us; the launch traced here: 55.5 us
  Pallas kernels  53.8 us (97%)
  local copies, waits for them, and re-layouts  1.02 us (2%)
  between operations  0.66 us (1%)
    pallas_call x1, Pallas kernels, on_device(): pl.pallas_call(kernel, out_shape=pltpu.VMEM(field.shape, field.dtype), in...  53.8 us

profile of v6, /device:TPU:192, one launch (start us, length us, event | category | flops | bytes accessed | tf_op | source)
XLA Modules:
  0.0 55.5 jit_solution(17618309115540948760)
XLA Ops:
  0.7 53.8 %shard_map.100 = f32[18,30,512]{2,1,0:T(8,128)S(1)} custom-call(f32[18,30,512]{2,1,0:T(8,128)} %field.1, f32[30]{0:T(128)} %speed_s.1, f32[8,128]{1,0:T(8,128)} %bitcast.5, f32[8,128]{1,0:T(8,128)} %bitcast.6, s32[2,1024]{1,0:T(2,128)} %cells_h.1, s32[1]{0:T(128)S(6)} %copy.13.live_s, s32[1,2,2]{2,1,0:T(2,128)} %table_h.1, s32[1,512]{1,0:T(1,128)} %bitcast.7, ...), custom_call_target="tpu_custom_call" | custom-call | tf_op jit(solution)/shard_map/pallas_call | solution.py:556
  54.4 1.0 %copy.12 = f32[18,30,512]{2,1,0:T(8,128)} copy(f32[18,30,512]{2,1,0:T(8,128)S(1)} %shard_map.100) | data formatting | bytes 2211840

commit v7 on v6

--- a/solution.py
+++ b/solution.py
@@ -14,7 +14,8 @@
 LANES = 128
 ROWS = 32
 CHUNKS = ((0, 1), (1, 2), (3, 2), (5, 2), (7, 1), (8, 1))
-AHEAD = 2
+LATE = 6
+AHEAD = 4
 EDGE_AT = 2
 PLANE = 32
 UP, DOWN = 7, 25
@@ -65,12 +66,15 @@
     picks,
     full,
     passing,
+    pass_full,
     load_sem,
     small_sem,
     table_send,
     table_recv,
     full_send,
     full_recv,
+    pass_full_send,
+    pass_full_recv,
     pass_send,
     pass_recv,
     send_sem,
@@ -199,12 +203,39 @@
             device_id_type=MESH,
         )
 
-    for side in (0, 1):
-
-        @pl.when(has[side])
+    def full_via(side, p):
+        return pltpu.make_async_remote_copy(
+            src_ref=cur.at[p],
+            dst_ref=pass_full.at[p],
+            send_sem=full_send.at[side, p],
+            recv_sem=pass_full_recv.at[p],
+            device_id=relay[side],
+            device_id_type=MESH,
+        )
+
+    beyond = (other(-DOWN - 1), other(PLANE - UP))
+
+    def full_pass(side, p):
+        return pltpu.make_async_remote_copy(
+            src_ref=pass_full.at[p],
+            dst_ref=full.at[1 - side, p],
+            send_sem=pass_full_send.at[p],
+            recv_sem=full_recv.at[1 - side, p],
+            device_id=beyond[side],
+            device_id_type=MESH,
+        )
+
+    for side in (0, 1):
+
+        @pl.when(has[side] & jnp.logical_not(via[side]))
         def _():
             for p in range(2 * AHEAD):
                 full_copy(side, p).start()
+
+        @pl.when(via[side])
+        def _():
+            for p in range(2 * AHEAD):
+                full_via(side, p).start()
 
     for copy in small[1:]:
         copy.wait()
@@ -317,44 +348,61 @@
             device_id_type=MESH,
         )
 
-    def via_copy(step, side, pair):
-        return pltpu.make_async_remote_copy(
-            src_ref=sent.at[step, side, pair],
-            dst_ref=passing.at[step, pair],
+    def via_copy(step, side, pair, e):
+        return pltpu.make_async_remote_copy(
+            src_ref=sent.at[step, side, pair, e],
+            dst_ref=passing.at[step, pair, e],
             send_sem=send_sem.at[step, side, pair],
-            recv_sem=pass_recv.at[step, pair],
+            recv_sem=pass_recv.at[step, pair, e],
             device_id=relay[side],
             device_id_type=MESH,
         )
 
-    def pass_copy(step, side, pair):
-        return pltpu.make_async_remote_copy(
-            src_ref=passing.at[step, pair],
-            dst_ref=got.at[step, 1 - side, pair],
-            send_sem=pass_send.at[step, pair],
+    def pass_copy(step, side, pair, e):
+        return pltpu.make_async_remote_copy(
+            src_ref=passing.at[step, pair, e],
+            dst_ref=got.at[step, 1 - side, pair, e],
+            send_sem=pass_send.at[step, pair, e],
             recv_sem=recv_sem.at[step, 1 - side, pair],
-            device_id=other(-DOWN - 1) if side == 0 else other(PLANE - UP),
-            device_id_type=MESH,
-        )
-
-    def pass_on(step, first):
+            device_id=beyond[side],
+            device_id_type=MESH,
+        )
+
+    def came(ref, send, recv):
+        pltpu.make_async_remote_copy(
+            src_ref=ref,
+            dst_ref=ref,
+            send_sem=send,
+            recv_sem=recv,
+            device_id=other(1),
+            device_id_type=MESH,
+        ).wait_recv()
+
+    def pass_on(step, first, last):
         for side, role in ((0, passes_down), (1, passes_up)):
 
             @pl.when(role)
             def _():
                 def one(pair, carry):
-                    pltpu.make_async_remote_copy(
-                        src_ref=passing.at[step, pair],
-                        dst_ref=passing.at[step, pair],
-                        send_sem=pass_send.at[step, pair],
-                        recv_sem=pass_recv.at[step, pair],
-                        device_id=other(1),
-                        device_id_type=MESH,
-                    ).wait_recv()
-                    pass_copy(step, side, pair).start()
+                    for e in (0, 1):
+                        came(
+                            passing.at[step, pair, e],
+                            pass_send.at[step, pair, e],
+                            pass_recv.at[step, pair, e],
+                        )
+                        pass_copy(step, side, pair, e).start()
                     return carry
 
-                lax.fori_loop(first, pairs, one, 0)
+                lax.fori_loop(first, last, one, 0)
+
+    def pass_full_on():
+        for side, role in ((0, passes_down), (1, passes_up)):
+
+            @pl.when(role)
+            def _():
+                for p in range(2 * AHEAD):
+                    came(pass_full.at[p], pass_full_send.at[p], pass_full_recv.at[p])
+                    full_pass(side, p).start()
 
     def halo_arrival(step, side, pair):
         return pltpu.make_async_remote_copy(
@@ -379,7 +427,8 @@
 
             @pl.when(via[side])
             def _():
-                via_copy(step, side, pair).start()
+                for e in (0, 1):
+                    via_copy(step, side, pair, e).start()
 
     home = {}
     for begin, count in CHUNKS:
@@ -401,7 +450,8 @@
         send_pair(0, pair)
     for p in range(dloc):
         split_own(p)
-    pass_on(0, AHEAD)
+    pass_full_on()
+    pass_on(0, AHEAD, pairs)
     for side in (0, 1):
 
         @pl.when(has[side])
@@ -491,7 +541,7 @@
     def one_step(step, carry):
         @pl.when(step > 0)
         def _():
-            pass_on(step, 0)
+            pass_on(step, 0, LATE)
 
         done = 1
         for chunk, (begin, count) in enumerate(CHUNKS):
@@ -499,6 +549,11 @@
             if chunk == 0:
                 edge_sent[step] = moved[0:2]
                 edge_copy(step).start()
+
+                @pl.when(step > 0)
+                def _():
+                    pass_on(step, LATE, pairs)
+
             if chunk == EDGE_AT:
                 edge_copy(step).wait_recv()
                 finish_pair(step, 0)
@@ -519,7 +574,10 @@
         def _():
             for step in range(ITERS):
                 for pair in range(AHEAD if step == 0 else 0, pairs):
-                    pass_copy(step, side, pair).wait_send()
+                    for e in (0, 1):
+                        pass_copy(step, side, pair, e).wait_send()
+            for p in range(2 * AHEAD):
+                full_pass(side, p).wait_send()
 
     for side in (0, 1):
 
@@ -595,14 +653,17 @@
             pltpu.VMEM((4 * hb, 8, LANES), jnp.int32),
             pltpu.VMEM((2, 2 * AHEAD, nfreq, own), F32),
             pltpu.VMEM((ITERS, pairs, 2, hb, nfreq, LANES), F32),
+            pltpu.VMEM((2 * AHEAD, nfreq, own), F32),
             pltpu.SemaphoreType.DMA((dloc,)),
             pltpu.SemaphoreType.DMA((7,)),
             pltpu.SemaphoreType.DMA((2,)),
             pltpu.SemaphoreType.DMA((2,)),
             pltpu.SemaphoreType.DMA((2, 2 * AHEAD)),
             pltpu.SemaphoreType.DMA((2, 2 * AHEAD)),
-            pltpu.SemaphoreType.DMA((ITERS, pairs)),
-            pltpu.SemaphoreType.DMA((ITERS, pairs)),
+            pltpu.SemaphoreType.DMA((2 * AHEAD,)),
+            pltpu.SemaphoreType.DMA((2 * AHEAD,)),
+            pltpu.SemaphoreType.DMA((ITERS, pairs, 2)),
+            pltpu.SemaphoreType.DMA((ITERS, pairs, 2)),
             pltpu.SemaphoreType.DMA((ITERS, 2, pairs)),
             pltpu.SemaphoreType.DMA((ITERS, 2, pairs)),
             pltpu.SemaphoreType.DMA((ITERS,)),

time: 55.6 us -> 57.2 us (1.029); the launches traced: 55.5 us -> 56.1 us
  Pallas kernels: 53.8 us -> 54.5 us
    pallas_call x1, Pallas kernels: 53.8 us -> 54.5 us  [on_device(): pl.pallas_call(kernel, out_shape=pltpu.VMEM(field.shape, field.dtype), in...]
where the time goes in v7:
time: 57.2 us; the launch traced here: 56.1 us
  Pallas kernels  54.5 us (95%)
  local copies, waits for them, and re-layouts  1.02 us (2%)
  between operations  0.66 us (1%)
    pallas_call x1, Pallas kernels, on_device(): pl.pallas_call(kernel, out_shape=pltpu.VMEM(field.shape, field.dtype), in...  54.5 us

profile of v7, /device:TPU:192, one launch (start us, length us, event | category | flops | bytes accessed | tf_op | source)
XLA Modules:
  0.0 56.1 jit_solution(767172720358535401)
XLA Ops:
  0.7 54.5 %shard_map.100 = f32[18,30,512]{2,1,0:T(8,128)S(1)} custom-call(f32[18,30,512]{2,1,0:T(8,128)} %field.1, f32[30]{0:T(128)} %speed_s.1, f32[8,128]{1,0:T(8,128)} %bitcast.5, f32[8,128]{1,0:T(8,128)} %bitcast.6, s32[2,1024]{1,0:T(2,128)} %cells_h.1, s32[1]{0:T(128)S(6)} %copy.13.live_s, s32[1,2,2]{2,1,0:T(2,128)} %table_h.1, s32[1,512]{1,0:T(1,128)} %bitcast.7, ...), custom_call_target="tpu_custom_call" | custom-call | tf_op jit(solution)/shard_map/pallas_call | solution.py:614
  55.1 1.0 %copy.12 = f32[18,30,512]{2,1,0:T(8,128)} copy(f32[18,30,512]{2,1,0:T(8,128)S(1)} %shard_map.100) | data formatting | bytes 2211840

commit v8 on v7

--- a/solution.py
+++ b/solution.py
@@ -15,7 +15,7 @@
 ROWS = 32
 CHUNKS = ((0, 1), (1, 2), (3, 2), (5, 2), (7, 1), (8, 1))
 LATE = 6
-AHEAD = 4
+AHEAD = 1
 EDGE_AT = 2
 PLANE = 32
 UP, DOWN = 7, 25

time: 57.2 us -> 58.3 us (1.019); the launches traced: 56.1 us -> 58.2 us
  Pallas kernels: 54.5 us -> 56.5 us
    pallas_call x1, Pallas kernels: 54.5 us -> 56.5 us  [on_device(): pl.pallas_call(kernel, out_shape=pltpu.VMEM(field.shape, field.dtype), in...]
where the time goes in v8:
time: 58.3 us; the launch traced here: 58.2 us
  Pallas kernels  56.5 us (97%)
  local copies, waits for them, and re-layouts  1.02 us (2%)
  between operations  0.66 us (1%)
    pallas_call x1, Pallas kernels, on_device(): pl.pallas_call(kernel, out_shape=pltpu.VMEM(field.shape, field.dtype), in...  56.5 us

profile of v8, /device:TPU:192, one launch (start us, length us, event | category | flops | bytes accessed | tf_op | source)
XLA Modules:
  0.0 58.2 jit_solution(9195548986326534421)
XLA Ops:
  0.7 56.5 %shard_map.100 = f32[18,30,512]{2,1,0:T(8,128)S(1)} custom-call(f32[18,30,512]{2,1,0:T(8,128)} %field.1, f32[30]{0:T(128)} %speed_s.1, f32[8,128]{1,0:T(8,128)} %bitcast.5, f32[8,128]{1,0:T(8,128)} %bitcast.6, s32[2,1024]{1,0:T(2,128)} %cells_h.1, s32[1]{0:T(128)S(6)} %copy.13.live_s, s32[1,2,2]{2,1,0:T(2,128)} %table_h.1, s32[1,512]{1,0:T(1,128)} %bitcast.7, ...), custom_call_target="tpu_custom_call" | custom-call | tf_op jit(solution)/shard_map/pallas_call | solution.py:614
  57.2 1.0 %copy.12 = f32[18,30,512]{2,1,0:T(8,128)} copy(f32[18,30,512]{2,1,0:T(8,128)S(1)} %shard_map.100) | data formatting | bytes 2211840

commit v9 on v8

--- a/solution.py
+++ b/solution.py
@@ -14,8 +14,8 @@
 LANES = 128
 ROWS = 32
 CHUNKS = ((0, 1), (1, 2), (3, 2), (5, 2), (7, 1), (8, 1))
-LATE = 6
-AHEAD = 1
+LATE = 9
+AHEAD = 2
 EDGE_AT = 2
 PLANE = 32
 UP, DOWN = 7, 25

time: 58.3 us -> 56.5 us (0.969)
  Pallas kernels: 56.5 us -> 54.6 us
    pallas_call x1, Pallas kernels: 56.5 us -> 54.6 us  [on_device(): pl.pallas_call(kernel, out_shape=pltpu.VMEM(field.shape, field.dtype), in...]
where the time goes in v9:
time: 56.5 us; the launch traced here: 56.3 us
  Pallas kernels  54.6 us (97%)
  local copies, waits for them, and re-layouts  1.02 us (2%)
  between operations  0.66 us (1%)
    pallas_call x1, Pallas kernels, on_device(): pl.pallas_call(kernel, out_shape=pltpu.VMEM(field.shape, field.dtype), in...  54.6 us

profile of v9, /device:TPU:192, one launch (start us, length us, event | category | flops | bytes accessed | tf_op | source)
XLA Modules:
  0.0 56.3 jit_solution(11155779877456897333)
XLA Ops:
  0.7 54.6 %shard_map.100 = f32[18,30,512]{2,1,0:T(8,128)S(1)} custom-call(f32[18,30,512]{2,1,0:T(8,128)} %field.1, f32[30]{0:T(128)} %speed_s.1, f32[8,128]{1,0:T(8,128)} %bitcast.5, f32[8,128]{1,0:T(8,128)} %bitcast.6, s32[2,1024]{1,0:T(2,128)} %cells_h.1, s32[1]{0:T(128)S(6)} %copy.13.live_s, s32[1,2,2]{2,1,0:T(2,128)} %table_h.1, s32[1,512]{1,0:T(1,128)} %bitcast.7, ...), custom_call_target="tpu_custom_call" | custom-call | tf_op jit(solution)/shard_map/pallas_call | solution.py:614
  55.3 1.0 %copy.12 = f32[18,30,512]{2,1,0:T(8,128)} copy(f32[18,30,512]{2,1,0:T(8,128)S(1)} %shard_map.100) | data formatting | bytes 2211840

commit v10 on v9

--- a/solution.py
+++ b/solution.py
@@ -14,7 +14,6 @@
 LANES = 128
 ROWS = 32
 CHUNKS = ((0, 1), (1, 2), (3, 2), (5, 2), (7, 1), (8, 1))
-LATE = 9
 AHEAD = 2
 EDGE_AT = 2
 PLANE = 32
@@ -66,15 +65,12 @@
     picks,
     full,
     passing,
-    pass_full,
     load_sem,
     small_sem,
     table_send,
     table_recv,
     full_send,
     full_recv,
-    pass_full_send,
-    pass_full_recv,
     pass_send,
     pass_recv,
     send_sem,
@@ -203,39 +199,14 @@
             device_id_type=MESH,
         )
 
-    def full_via(side, p):
-        return pltpu.make_async_remote_copy(
-            src_ref=cur.at[p],
-            dst_ref=pass_full.at[p],
-            send_sem=full_send.at[side, p],
-            recv_sem=pass_full_recv.at[p],
-            device_id=relay[side],
-            device_id_type=MESH,
-        )
-
     beyond = (other(-DOWN - 1), other(PLANE - UP))
 
-    def full_pass(side, p):
-        return pltpu.make_async_remote_copy(
-            src_ref=pass_full.at[p],
-            dst_ref=full.at[1 - side, p],
-            send_sem=pass_full_send.at[p],
-            recv_sem=full_recv.at[1 - side, p],
-            device_id=beyond[side],
-            device_id_type=MESH,
-        )
-
-    for side in (0, 1):
-
-        @pl.when(has[side] & jnp.logical_not(via[side]))
+    for side in (0, 1):
+
+        @pl.when(has[side])
         def _():
             for p in range(2 * AHEAD):
                 full_copy(side, p).start()
-
-        @pl.when(via[side])
-        def _():
-            for p in range(2 * AHEAD):
-                full_via(side, p).start()
 
     for copy in small[1:]:
         copy.wait()
@@ -395,15 +366,6 @@
 
                 lax.fori_loop(first, last, one, 0)
 
-    def pass_full_on():
-        for side, role in ((0, passes_down), (1, passes_up)):
-
-            @pl.when(role)
-            def _():
-                for p in range(2 * AHEAD):
-                    came(pass_full.at[p], pass_full_send.at[p], pass_full_recv.at[p])
-                    full_pass(side, p).start()
-
     def halo_arrival(step, side, pair):
         return pltpu.make_async_remote_copy(
             src_ref=sent.at[step, side, pair],
@@ -450,7 +412,6 @@
         send_pair(0, pair)
     for p in range(dloc):
         split_own(p)
-    pass_full_on()
     pass_on(0, AHEAD, pairs)
     for side in (0, 1):
 
@@ -541,7 +502,7 @@
     def one_step(step, carry):
         @pl.when(step > 0)
         def _():
-            pass_on(step, 0, LATE)
+            pass_on(step, 0, pairs)
 
         done = 1
         for chunk, (begin, count) in enumerate(CHUNKS):
@@ -549,11 +510,6 @@
             if chunk == 0:
                 edge_sent[step] = moved[0:2]
                 edge_copy(step).start()
-
-                @pl.when(step > 0)
-                def _():
-                    pass_on(step, LATE, pairs)
-
             if chunk == EDGE_AT:
                 edge_copy(step).wait_recv()
                 finish_pair(step, 0)
@@ -576,8 +532,6 @@
                 for pair in range(AHEAD if step == 0 else 0, pairs):
                     for e in (0, 1):
                         pass_copy(step, side, pair, e).wait_send()
-            for p in range(2 * AHEAD):
-                full_pass(side, p).wait_send()
 
     for side in (0, 1):
 
@@ -653,15 +607,12 @@
             pltpu.VMEM((4 * hb, 8, LANES), jnp.int32),
             pltpu.VMEM((2, 2 * AHEAD, nfreq, own), F32),
             pltpu.VMEM((ITERS, pairs, 2, hb, nfreq, LANES), F32),
-            pltpu.VMEM((2 * AHEAD, nfreq, own), F32),
             pltpu.SemaphoreType.DMA((dloc,)),
             pltpu.SemaphoreType.DMA((7,)),
             pltpu.SemaphoreType.DMA((2,)),
             pltpu.SemaphoreType.DMA((2,)),
             pltpu.SemaphoreType.DMA((2, 2 * AHEAD)),
             pltpu.SemaphoreType.DMA((2, 2 * AHEAD)),
-            pltpu.SemaphoreType.DMA((2 * AHEAD,)),
-            pltpu.SemaphoreType.DMA((2 * AHEAD,)),
             pltpu.SemaphoreType.DMA((ITERS, pairs, 2)),
             pltpu.SemaphoreType.DMA((ITERS, pairs, 2)),
             pltpu.SemaphoreType.DMA((ITERS, 2, pairs)),

time: 56.5 us -> 56.4 us (level)
  no operation moved by 1% of the time
where the time goes in v10:
time: 56.4 us; the launch traced here: 56.2 us
  Pallas kernels  54.6 us (97%)
  local copies, waits for them, and re-layouts  1.02 us (2%)
  between operations  0.66 us (1%)
    pallas_call x1, Pallas kernels, on_device(): pl.pallas_call(kernel, out_shape=pltpu.VMEM(field.shape, field.dtype), in...  54.6 us

profile of v10, /device:TPU:192, one launch (start us, length us, event | category | flops | bytes accessed | tf_op | source)
XLA Modules:
  0.0 56.2 jit_solution(6258308400414445847)
XLA Ops:
  0.7 54.6 %shard_map.100 = f32[18,30,512]{2,1,0:T(8,128)S(1)} custom-call(f32[18,30,512]{2,1,0:T(8,128)} %field.1, f32[30]{0:T(128)} %speed_s.1, f32[8,128]{1,0:T(8,128)} %bitcast.5, f32[8,128]{1,0:T(8,128)} %bitcast.6, s32[2,1024]{1,0:T(2,128)} %cells_h.1, s32[1]{0:T(128)S(6)} %copy.13.live_s, s32[1,2,2]{2,1,0:T(2,128)} %table_h.1, s32[1,512]{1,0:T(1,128)} %bitcast.7, ...), custom_call_target="tpu_custom_call" | custom-call | tf_op jit(solution)/shard_map/pallas_call | solution.py:568
  55.2 1.0 %copy.12 = f32[18,30,512]{2,1,0:T(8,128)} copy(f32[18,30,512]{2,1,0:T(8,128)S(1)} %shard_map.100) | data formatting | bytes 2211840

commit v11 on v6

--- a/solution.py
+++ b/solution.py
@@ -15,7 +15,7 @@
 ROWS = 32
 CHUNKS = ((0, 1), (1, 2), (3, 2), (5, 2), (7, 1), (8, 1))
 AHEAD = 2
-EDGE_AT = 2
+EDGE_AT = 1
 PLANE = 32
 UP, DOWN = 7, 25
 HOT = jnp.float8_e4m3fn

time: 55.6 us -> 58.3 us (1.049)
  Pallas kernels: 53.8 us -> 56.4 us
    pallas_call x1, Pallas kernels: 53.8 us -> 56.4 us  [on_device(): pl.pallas_call(kernel, out_shape=pltpu.VMEM(field.shape, field.dtype), in...]
where the time goes in v11:
time: 58.3 us; the launch traced here: 58.1 us
  Pallas kernels  56.4 us (97%)
  local copies, waits for them, and re-layouts  1.02 us (2%)
  between operations  0.66 us (1%)
    pallas_call x1, Pallas kernels, on_device(): pl.pallas_call(kernel, out_shape=pltpu.VMEM(field.shape, field.dtype), in...  56.4 us

profile of v11, /device:TPU:192, one launch (start us, length us, event | category | flops | bytes accessed | tf_op | source)
XLA Modules:
  0.0 58.1 jit_solution(12186901213004004844)
XLA Ops:
  0.7 56.4 %shard_map.100 = f32[18,30,512]{2,1,0:T(8,128)S(1)} custom-call(f32[18,30,512]{2,1,0:T(8,128)} %field.1, f32[30]{0:T(128)} %speed_s.1, f32[8,128]{1,0:T(8,128)} %bitcast.5, f32[8,128]{1,0:T(8,128)} %bitcast.6, s32[2,1024]{1,0:T(2,128)} %cells_h.1, s32[1]{0:T(128)S(6)} %copy.13.live_s, s32[1,2,2]{2,1,0:T(2,128)} %table_h.1, s32[1,512]{1,0:T(1,128)} %bitcast.7, ...), custom_call_target="tpu_custom_call" | custom-call | tf_op jit(solution)/shard_map/pallas_call | solution.py:556
  57.1 1.0 %copy.12 = f32[18,30,512]{2,1,0:T(8,128)} copy(f32[18,30,512]{2,1,0:T(8,128)S(1)} %shard_map.100) | data formatting | bytes 2211840
